TPU v7x, 128 devices: a whole 4x4x4 slice. The times are simulated.
128 devices in a mesh: sx: 8 (over x, core), sy: 8 (over z, y_hi), dp: 2 (over y_lo).
Axes of the slice: x: 4, y: 4 (y_hi: 2, y_lo: 2; y = y_hi * 2 + y_lo), z: 4, core: 2. Of those that a mesh axis runs over, the one named last changes fastest.
Arguments:
- tokens: bfloat16 [2, 32768, 1280], P('dp', ('sx', 'sy')), may hold values from -6 to 6
- lengths: int32 [2, 256], P('dp'), may hold values from 1 to 512, 32768 in all within a row
- ln_gain: float32 [1280], replicated, may hold values from 0.1 to 1.9
- w_qkv: bfloat16 [1280, 3840], P('dp'), may hold values from -4 to 4, as said below
- w_out: bfloat16 [1280, 1280], P('dp'), may hold values from -0.15625 to 0.15625
Outputs:
- hidden: bfloat16 [2, 32768, 1280], P('dp', ('sx', 'sy'))
- pooled: float32 [2, 256, 1280], P('dp')
Inputs may be any that keep to these rules, and one draw needn't show every extreme that they name: The 256 lengths of a row sum to 32768; images are packed end to end in order. `w_qkv`: columns are queries, then keys, then values, each of 16 heads of 80 columns.
All inputs are finite; a program needn't handle non-finite values.
Results may differ from a plain program's by a relative error of at most 0.0051.
Values may be sent and summed in bfloat16 or wider, within the bound.
A program may use at most 128 MiB of HBM per device.

v0:
```python
import jax
import jax.numpy as jnp
from jax import lax
from jax.sharding import PartitionSpec as P

HEADS = 16
MAXLEN = 512


def from_everyone(shard, axis):
    length = lax.axis_size(axis)
    return lax.all_to_all(
        jnp.broadcast_to(shard[None], (length, *shard.shape)), axis, 0, 0, tiled=True
    )


def laid_out(pieces, dim):
    pieces = jnp.moveaxis(pieces, 0, dim)
    dims = pieces.shape
    return pieces.reshape(*dims[:dim], dims[dim] * dims[dim + 1], *dims[dim + 2 :])


def gather_directly(shard, axis, dim):
    pieces = from_everyone(shard, axis)
    return laid_out(pieces, dim)


def side_by_side(arrays, axis, dim, along):
    both = jnp.concatenate(arrays, axis=along)
    result, at, gathered = (gather_directly(both, axis, dim), 0, [])
    for a in arrays:
        gathered.append(lax.slice_in_dim(result, at, at + a.shape[along], axis=along))
        at += a.shape[along]
    return tuple(gathered)


def with_halo(shard, sides, width):
    edges = {}
    for axis, dim in sides:
        size, length = (lax.axis_size(axis), shard.shape[dim])
        up = [(i, (i + 1) % size) for i in range(size - 1)]
        last = lax.slice_in_dim(shard, length - width, length, axis=dim)
        initial = lax.slice_in_dim(shard, 0, width, axis=dim)
        edges[dim] = (
            lax.ppermute(last, axis, up),
            lax.ppermute(initial, axis, [(b, a) for a, b in up]),
        )
    done = []
    for _, dim in sides:
        low, high = edges[dim]
        around = [(width, width) if d in done else (0, 0) for d in range(shard.ndim)]
        shard = jnp.concatenate([jnp.pad(low, around), shard, jnp.pad(high, around)], axis=dim)
        done.append(dim)
    return shard


def split_up(shard, dim, length):
    dims = shard.shape
    pieces = shard.reshape(*dims[:dim], length, dims[dim] // length, *dims[dim + 1 :])
    return jnp.moveaxis(pieces, dim, 0)


def sent_and_summed(shard, axis, dim):
    pieces = split_up(shard, dim, lax.axis_size(axis))
    arrived = lax.all_to_all(pieces, axis, split_axis=0, concat_axis=0, tiled=True)
    return arrived.sum(axis=0)


def filled_up(lines, length):
    spare = -len(lines) % length
    return jnp.pad(lines, [(0, spare)] + [(0, 0)] * (lines.ndim - 1))


def total_of(shard, axes):
    lines = shard.reshape(-1, shard.shape[-1])
    own = sent_and_summed(filled_up(lines, lax.axis_size(axes)), axes, 0)
    whole = gather_directly(own, axes, 0)
    return whole[: len(lines)].reshape(shard.shape)


def image_ids(lengths, positions, total):
    offsets = jnp.cumsum(lengths) - lengths
    counted = jnp.sum((offsets[None, :] <= positions[:, None]).astype(jnp.int32), axis=1) - 1
    inside = (positions >= 0) & (positions < total)
    return jnp.where(inside, counted, -1)


def normalize(rows, ln_gain):
    values = rows.astype(jnp.float32)
    center = values - jnp.mean(values, axis=-1, keepdims=True)
    spread = jnp.mean(center * center, axis=-1, keepdims=True)
    return (center * lax.rsqrt(spread + 1e-05) * ln_gain).astype(jnp.bfloat16)


def attend(queries, keys, values, q_ids, k_ids):
    length = queries.shape[0]
    heads = queries.shape[1]
    block = min(512, length)
    scale = queries.shape[2] ** (-0.5)

    def one_block(index):
        allowed = q_ids[:, None] == k_ids[None, :]

        def one_head(head):
            q_head = lax.dynamic_index_in_dim(queries, head, 1, keepdims=False)
            k_head = lax.dynamic_index_in_dim(keys, head, 1, keepdims=False)
            v_head = lax.dynamic_index_in_dim(values, head, 1, keepdims=False)
            scores = jnp.dot(q_head, k_head.T, preferred_element_type=jnp.float32) * scale
            scores = jnp.where(allowed, scores, -1e30)
            top = jnp.max(scores, axis=1, keepdims=True)
            weights = jnp.exp(scores - top)
            probs = (weights / jnp.sum(weights, axis=1, keepdims=True)).astype(jnp.bfloat16)
            return jnp.dot(probs, v_head, preferred_element_type=jnp.float32).astype(jnp.bfloat16)

        outcome = lax.map(one_head, jnp.arange(heads, dtype=jnp.int32))
        return jnp.transpose(outcome, (1, 0, 2))

    blocks = lax.map(one_block, jnp.arange(length // block, dtype=jnp.int32))
    return blocks.reshape(length, heads, -1)


def shards(tokens, lengths, ln_gain, w_qkv, w_out):
    qkv_full, out_full = side_by_side((w_qkv, w_out), "dp", 0, 1)
    count_rows = tokens.shape[0]
    local = tokens.shape[1]
    width = tokens.shape[2]
    size = width // HEADS
    images = lengths.shape[1]
    count_x = lax.axis_size("sx")
    count_y = lax.axis_size("sy")
    total = local * count_x * count_y
    shard = lax.axis_index("sx") * count_y + lax.axis_index("sy")
    own_positions = shard * local + jnp.arange(local, dtype=jnp.int32)
    own_list = [image_ids(lengths[0], own_positions, total)]
    normed = normalize(tokens, ln_gain)
    qkv = jnp.dot(
        normed.reshape(count_rows * local, width), qkv_full, preferred_element_type=jnp.float32
    )
    qkv = qkv.astype(jnp.bfloat16).reshape(count_rows, local, 3 * width)
    pieces = qkv.reshape(count_rows, local, 3, HEADS, size)
    keyvals = with_halo(pieces[:, :, 1:3], ((("sx", "sy"), 1),), MAXLEN)
    k_pos = shard * local - MAXLEN + jnp.arange(local + 2 * MAXLEN, dtype=jnp.int32)
    rowidx = 0
    k_ids = image_ids(lengths[rowidx], k_pos, total)
    outcomes = [
        attend(
            pieces[rowidx, :, 0],
            keyvals[rowidx, :, 0],
            keyvals[rowidx, :, 1],
            own_list[rowidx],
            k_ids,
        )
    ]
    context = jnp.stack(outcomes, axis=0).reshape(count_rows * local, width)
    mixed = jnp.dot(context, out_full, preferred_element_type=jnp.float32).reshape(
        count_rows, local, width
    )
    hidden = (tokens.astype(jnp.float32) + mixed).astype(jnp.bfloat16)
    labels = jnp.arange(images, dtype=jnp.int32)
    rowidx = 0
    onehot = (labels[:, None] == own_list[rowidx][None, :]).astype(jnp.bfloat16)
    parts_list = [jnp.dot(onehot, hidden[rowidx], preferred_element_type=jnp.float32)]
    terms = jnp.stack(parts_list, axis=0)
    sums = total_of(terms, ("sx", "sy"))
    pooled = sums / lengths.astype(jnp.float32)[:, :, None]
    return (hidden, pooled)


def solution(mesh):
    in_specs = (P("dp", ("sx", "sy"), None), P("dp", None), P(), P("dp", None), P("dp", None))
    out_specs = (P("dp", ("sx", "sy"), None), P("dp", None, None))
    return jax.shard_map(shards, mesh=mesh, in_specs=in_specs, out_specs=out_specs, check_vma=False)
```

profile of v0, /device:TPU:1, one launch (start us, length us, event | category | flops | bytes accessed | tf_op | source)
XLA Modules:
  0.0 480.5 jit_solution(12452729132204188104)
XLA Ops:
  0.6 3.7 pad_maximum_fusion.1
  4.3 5.4 %broadcast_in_dim.18 = bf16[2,640,5120]{2,1,0:T(8,128)(2,1)} broadcast(bf16[640,5120]{1,0:T(8,128)(2,1)S(1)} %pad_maximum_fusion.1), dimensions={1,2} | broadcast | bytes 19660800 | tf_op jit(solution)/shard_map/broadcast_in_dim | solution.py:13
  9.7 8.7 %all-to-all-start = ((bf16[2,640,5120]{2,1,0:T(8,128)(2,1)}), bf16[2,640,5120]{2,1,0:T(8,128)(2,1)}, u32[]{:S(2)}, u32[]{:S(2)}) async-start(bf16[2,640,5120]{2,1,0:T(8,128)(2,1)} %broadcast_in_dim.18), calls=%async_computation | async-start | bytes 26214400 | tf_op jit(solution)/shard_map/all_to_all | solution.py:12
  19.2 142.1 %all-to-all-done = bf16[2,640,5120]{2,1,0:T(8,128)(2,1)} async-done(((bf16[2,640,5120]{2,1,0:T(8,128)(2,1)}), bf16[2,640,5120]{2,1,0:T(8,128)(2,1)}, u32[]{:S(2)}, u32[]{:S(2)}) %all-to-all-start) | async-done | bytes 13107232 | tf_op jit(solution)/shard_map/all_to_all | solution.py:12
  161.3 10.8 %fusion.18 = bf16[512,3840]{1,0:T(8,128)(2,1)} fusion(bf16[1280,5120]{1,0:T(8,128)(2,1)} %bitcast.1, bf16[1,512,1280]{2,1,0:T(8,128)(2,1)S(1)} %copy-done, f32[1280]{0:T(1024)S(1)} %copy-done.4, f32[512]{0:T(512)S(1)} %add_rsqrt_fusion, f32[512]{0:T(512)S(1)} %broadcast_multiply_fusion), kind=kOutput, calls=%fused_computation.22 | convolution fusion | flops 5038407680 | bytes 15082496 | tf_op jit(solution)/shard_map/dot_general | solution.py:136
  172.1 6.2 %copy.12 = bf16[512,3840]{0,1:T(8,128)(2,1)} copy(bf16[512,3840]{1,0:T(8,128)(2,1)} %fusion.18) | data formatting | bytes 7864320 | tf_op jit(solution)/shard_map/convert_element_type | solution.py:139
  178.3 1.9 slice.35
  180.3 10.0 %collective-permute-start.1 = (bf16[1,512,2,16,80]{1,4,3,2,0:T(8,128)(2,1)S(1)}, bf16[1,512,2,16,80]{1,4,3,2,0:T(8,128)(2,1)}, u32[]{:S(2)}, u32[]{:S(2)}) collective-permute-start(bf16[1,512,2,16,80]{1,4,3,2,0:T(8,128)(2,1)S(1)} %slice.35), channel_id=1, source_target_pairs={{2,0},{4,2},{6,4},{8,6},{10,8},{12,10},{14,12},{16,14},{18,16},{20... | collective-permute-start | bytes 7864328 | tf_op jit(solution)/shard_map/ppermute | solution.py:46
  190.3 1.9 collective-permute-start
  193.6 2.5 slice_bitcast_fusion.2
  196.1 78.1 %collective-permute-done.1 = bf16[1,512,2,16,80]{1,4,3,2,0:T(8,128)(2,1)} collective-permute-done((bf16[1,512,2,16,80]{1,4,3,2,0:T(8,128)(2,1)S(1)}, bf16[1,512,2,16,80]{1,4,3,2,0:T(8,128)(2,1)}, u32[]{:S(2)}, u32[]{:S(2)}) %collective-permute-start.1) | collective-permute-done | bytes 2621472 | tf_op jit(solution)/shard_map/ppermute | solution.py:46
  274.2 28.1 %collective-permute-done = bf16[1,512,2,16,80]{1,4,3,2,0:T(8,128)(2,1)} collective-permute-done((bf16[1,512,2,16,80]{1,4,3,2,0:T(8,128)(2,1)S(1)}, bf16[1,512,2,16,80]{1,4,3,2,0:T(8,128)(2,1)}, u32[]{:S(2)}, u32[]{:S(2)}) %collective-permute-start) | collective-permute-done | bytes 2621472 | tf_op jit(solution)/shard_map/ppermute | solution.py:45
  302.3 3.4 pad_maximum_fusion
  305.7 3.4 slice_bitcast_fusion
  309.1 106.8 %while.18 = (s32[]{:T(128)}, bf16[16,512,80]{1,2,0:T(8,128)(2,1)S(1)}, s32[16]{0:T(128)S(1)}, bf16[512,16,80]{0,2,1:T(8,128)(2,1)}, bf16[1536,16,80]{0,2,1:T(8,1...) while((s32[]{:T(128)}, ...), condition=%wide.region_9.10_spmd.clone, body=%wide.region_6.9_spmd.clone.sunk | while | flops 258776064 | bytes 10112171 | solution.py:115
  327.3 1.8 fusion.56
  334.0 1.8 fusion.56
  354.0 1.8 fusion.56
  360.7 1.8 fusion.56
  380.8 1.8 fusion.56
  387.4 1.8 fusion.56
  416.0 3.8 fusion.30
  421.2 31.1 %all_to_all.15 = f32[64,4,1280]{2,1,0:T(4,128)S(1)} all-to-all(f32[64,4,1280]{2,1,0:T(4,128)S(1)} %copy.13), channel_id=1, replica_groups=mesh['sx'=8,'sy'=8,'dp'=2] {'sx','sy'}, dimensions={0} | all-to-all | bytes 2621440 | tf_op jit(solution)/shard_map/all_to_all | solution.py:65
  452.7 26.1 %all_to_all.16 = f32[64,4,1280]{2,1,0:T(4,128)S(1)} all-to-all(f32[64,4,1280]{2,1,0:T(4,128)S(1)} %broadcast_in_dim.20), channel_id=1, replica_groups=mesh['sx'=8,'sy'=8,'dp'=2] {'sx','sy'}, dimensions={0} | all-to-all | bytes 2621440 | tf_op jit(solution)/shard_map/all_to_all | solution.py:12
  (95 shorter events, 70.3 us)
Async XLA Ops:
  9.7 8.7 %copy-start = (bf16[1,512,1280]{2,1,0:T(8,128)(2,1)S(1)}, bf16[1,512,1280]{2,1,0:T(8,128)(2,1)}, u32[]{:S(2)}) copy-start(bf16[1,512,1280]{2,1,0:T(8,128)(2,1)} %param.7) | copy-start | bytes 3932164
  9.7 151.5 %all-to-all-start = ((bf16[2,640,5120]{2,1,0:T(8,128)(2,1)}), bf16[2,640,5120]{2,1,0:T(8,128)(2,1)}, u32[]{:S(2)}, u32[]{:S(2)}) async-start(bf16[2,640,5120]{2,1,0:T(8,128)(2,1)} %broadcast_in_dim.18), calls=%async_computation | async-start | bytes 26214400 | tf_op jit(solution)/shard_map/all_to_all | solution.py:12
  18.4 142.8 %copy-start.4 = (f32[1280]{0:T(1024)S(1)}, f32[1280]{0:T(1024)}, u32[]{:S(2)}) copy-start(f32[1280]{0:T(1024)} %param.9) | copy-start | bytes 15364
  178.3 13.9 %copy-start.3 = (s32[1,256]{1,0:T(1,128)S(1)}, s32[1,256]{1,0:T(1,128)}, u32[]{:S(2)}) copy-start(s32[1,256]{1,0:T(1,128)} %param.8) | copy-start | bytes 3076
  180.3 93.9 %collective-permute-start.1 = (bf16[1,512,2,16,80]{1,4,3,2,0:T(8,128)(2,1)S(1)}, bf16[1,512,2,16,80]{1,4,3,2,0:T(8,128)(2,1)}, u32[]{:S(2)}, u32[]{:S(2)}) collective-permute-start(bf16[1,512,2,16,80]{1,4,3,2,0:T(8,128)(2,1)S(1)} %slice.35), channel_id=1, source_target_pairs={{2,0},{4,2},{6,4},{8,6},{10,8},{12,10},{14,12},{16,14},{18,16},{20... | collective-permute-start | bytes 7864328 | tf_op jit(solution)/shard_map/ppermute | solution.py:46
  190.3 112.0 %collective-permute-start = (bf16[1,512,2,16,80]{1,4,3,2,0:T(8,128)(2,1)S(1)}, bf16[1,512,2,16,80]{1,4,3,2,0:T(8,128)(2,1)}, u32[]{:S(2)}, u32[]{:S(2)}) collective-permute-start(bf16[1,512,2,16,80]{1,4,3,2,0:T(8,128)(2,1)S(1)} %slice.35), channel_id=1, source_target_pairs={{0,2},{2,4},{4,6},{6,8},{8,10},{10,12},{12,14},{14,16},{16,18},{18... | collective-permute-start | bytes 7864328 | tf_op jit(solution)/shard_map/ppermute | solution.py:45
  305.7 3.4 copy-start.5
  309.1 106.9 %copy-start.1 = (bf16[1,512,1280]{2,1,0:T(8,128)(2,1)S(1)}, bf16[1,512,1280]{2,1,0:T(8,128)(2,1)}, u32[]{:S(2)}) copy-start(bf16[1,512,1280]{2,1,0:T(8,128)(2,1)} %param.7) | copy-start | bytes 3932164
  419.8 1.4 copy-start.2
where the time goes:
time: 482 us; the launch traced here: 480 us
  waiting for transfers between devices  248 us (51%)
  matrix products  72.2 us (15%)
  blocking collectives  57.2 us (12%)
  loops' own time  31.3 us (6%)
  local copies, waits for them, and re-layouts  30.5 us (6%)
  starting transfers between devices  20.6 us (4%)
  other arithmetic  19.6 us (4%)
    all_to_all x1, waiting for transfers between devices, from_everyone(): lax.all_to_all(jnp.broadcast_to(shard[None], (length, *shard.shape)), axi...  142 us
    ppermute x1, waiting for transfers between devices, with_halo(): lax.ppermute(initial, axis, [(b, a) for a, b in up])  78.1 us
    another operation x1, loops' own time, one_block(): outcome = lax.map(one_head, jnp.arange(heads, dtype=jnp.int32))  31.3 us
    all_to_all x1, blocking collectives, sent_and_summed(): lax.all_to_all(pieces, axis, split_axis=0, concat_axis=0, tiled=True)  31.1 us
    dot_general x16, matrix products, one_head(): jnp.dot(probs, v_head, preferred_element_type=jnp.float32)  28.8 us
    dot_general x16, matrix products, one_head(): jnp.dot(q_head, k_head.T, preferred_element_type=jnp.float32) * scale  28.1 us
    ppermute x1, waiting for transfers between devices, with_halo(): lax.ppermute(last, axis, up)  28.1 us
    all_to_all x1, blocking collectives, from_everyone(): lax.all_to_all(jnp.broadcast_to(shard[None], (length, *shard.shape)), axi...  26.1 us
  transfers between devices with their start and end apart: 3, of which 3 were waited for; matrix products, arithmetic and copies ran while one was open for 1% of the time, Pallas kernels for 0%

commit v1 on v0

v1 whole, which is shorter than its diff:
```python
import math

import jax
import jax.numpy as jnp
from jax import lax
from jax.experimental import pallas as pl
from jax.experimental.pallas import tpu as pltpu
from jax.sharding import PartitionSpec as P

MESH = pl.DeviceIdType.MESH
F32 = jnp.float32
BF16 = jnp.bfloat16
D = 1280
HALF = 640
N = 512
SIZE = 80
IMAGES = 256
TOTAL = 32768
SCALE = SIZE**-0.5 * math.log2(math.e)
PIECE = 80
CLASSES = (2, 3, 4, 5, 6, 9)
VMEM_LIMIT = 62 * 1024 * 1024


def places():
    sx, sy, d = lax.axis_index("sx"), lax.axis_index("sy"), lax.axis_index("dp")
    h = lax.rem(sy, 2)
    flip = sy + 1 - 2 * h
    shard = sx * 8 + sy
    onward = lax.rem(shard + 2 - 4 * h + 64, 64)
    back = lax.rem(shard - 2 + 4 * h + 64, 64)
    mate = sx + 1 - 2 * lax.rem(sx, 2)
    where = {
        "a": (sx, sy, 1 - d),
        "b": (sx, flip, 1 - d),
        "xp": (lax.rem(sx + 2, 8), sy, d),
        "xm": (lax.rem(sx + 6, 8), sy, d),
        "core": (mate, sy, d),
        "z": (onward // 8, lax.rem(onward, 8), d),
        "zb": (back // 8, lax.rem(back, 8), d),
    }
    return sx, sy, d, h, mate, where


def normalize(rows, gain):
    values = rows.astype(F32)
    center = values - jnp.mean(values, axis=-1, keepdims=True)
    spread = jnp.mean(center * center, axis=-1, keepdims=True)
    return (center * lax.rsqrt(spread + 1e-05) * gain).astype(BF16)


class Exchange:
    def __init__(self, own, other, width, sx, mate, where, send, recv):
        self.own, self.other, self.width = own, other, width
        self.sx, self.mate, self.where = sx, mate, where
        self.send, self.recv = send, recv
        self.started = []

    def rows(self, owner):
        return pl.ds(pl.multiple_of(lax.rem(owner + 8, 8) * PIECE, 16), PIECE)

    def copy(self, i, src, owner, cols, to):
        rows = self.rows(owner)
        return pltpu.make_async_remote_copy(
            src_ref=src.at[rows, cols],
            dst_ref=self.other.at[rows, cols],
            send_sem=self.send.at[i],
            recv_sem=self.recv.at[i],
            device_id=self.where[to],
            device_id_type=MESH,
        )

    def describe(self, i):
        sx, w = self.sx, self.width
        low, high, full = pl.ds(0, w // 2), pl.ds(w // 2, w // 2), pl.ds(0, w)
        table = (
            (self.own, sx, low, "a"),
            (self.own, sx, high, "b"),
            (self.other, sx, full, "xp"),
            (self.other, sx, full, "xm"),
            (self.other, sx, full, "core"),
            (self.other, sx + 2, low, "xm"),
            (self.other, sx + 2, full, "core"),
            (self.other, sx - 2, high, "xp"),
            (self.other, sx - 2, full, "core"),
            (self.other, sx + 4, full, "core"),
        )
        return self.copy(i, *table[i])

    def go(self, *which):
        for i in which:
            self.describe(i).start()

    def arrived(self, *which):
        for i in which:
            self.describe(i).wait_recv()

    def sent(self):
        for i in range(10):
            self.describe(i).wait_send()


def gather_kernel(
    tok_hbm, gain_ref, wq_hbm, wo_hbm,
    q_out, k_out, v_out, wo_out,
    tok, wq, wqo, woo, near, far, ta, tb, nrm, nrm2, acc, qs, ks, vs,
    wq_send, wq_recv, wo_send, wo_recv, h_send, h_recv, local,
):
    sx, sy, d, h, mate, where = places()
    barrier = pltpu.get_barrier_semaphore()
    for name in ("a", "b", "xp", "xm", "core", "z", "zb"):
        pl.semaphore_signal(barrier, inc=1, device_id=where[name], device_id_type=MESH)

    tok_in = pltpu.make_async_copy(tok_hbm, tok, local.at[0])
    wq_in = pltpu.make_async_copy(wq_hbm, wq, local.at[1])
    tok_in.start()
    wq_in.start()
    pl.semaphore_wait(barrier, 7)

    big = Exchange(wq_hbm, wqo, 3 * D, sx, mate, where, wq_send, wq_recv)
    small = Exchange(wo_hbm, woo, D, sx, mate, where, wo_send, wo_recv)

    def chunk(i):
        return pl.ds(128 * i, 128)

    table = (
        (tok_hbm, 0, ta, 0, "a"),
        (tok_hbm, 1, ta, 1, "a"),
        (tok_hbm, 2, tb, 0, "b"),
        (tok_hbm, 3, tb, 1, "b"),
        (ta, 0, near, 0, "b"),
        (ta, 1, near, 1, "b"),
        (tb, 0, near, 2, "a"),
        (tb, 1, near, 3, "a"),
        (near, 0, far, 0, "z"),
        (near, 2, far, 2, "z"),
        (near, 1, far, 1, "z"),
        (near, 3, far, 3, "z"),
    )

    def halo(i):
        src, at, dst, to, name = table[i]
        return pltpu.make_async_remote_copy(
            src_ref=src.at[chunk(at)],
            dst_ref=dst.at[chunk(to)],
            send_sem=h_send.at[i],
            recv_sem=h_recv.at[i],
            device_id=where[name],
            device_id_type=MESH,
        )

    big.go(0, 1)
    for i in (0, 2, 1, 3):
        halo(i).start()
    small.go(0, 1)

    gain = gain_ref[...]
    mine = pl.ds(pl.multiple_of(d * HALF, 128), HALF)
    others = pl.ds(pl.multiple_of((1 - d) * HALF, 128), HALF)

    tok_in.wait()

    def norm_own(i, _):
        rows = pl.ds(pl.multiple_of(i * 64, 64), 64)
        nrm[rows, :] = normalize(tok[rows, :], gain)
        return 0

    lax.fori_loop(0, N // 64, norm_own, 0)
    wq_in.wait()

    def first_half(i, _):
        rows = pl.ds(pl.multiple_of(i * 256, 256), 256)
        for part in range(3):
            cols = pl.ds(part * D, D)
            acc[rows, cols] = jnp.dot(nrm[rows, mine], wq[:, cols], preferred_element_type=F32)
        return 0

    lax.fori_loop(0, 2, first_half, 0)

    big.arrived(0, 1)
    big.go(2, 3, 4)
    for i, j in ((0, 4), (2, 6)):
        halo(i).wait_recv()
        halo(j).start()
    big.arrived(3)
    big.go(5, 6)
    big.arrived(2)
    big.go(7, 8)
    for i, j in ((1, 5), (3, 7)):
        halo(i).wait_recv()
        halo(j).start()
    small.arrived(0, 1)
    small.go(2, 3, 4)
    big.arrived(5, 7)
    big.go(9)
    big.arrived(4, 6, 8, 9)

    def second_half(i, _):
        rows = pl.ds(pl.multiple_of(i * 256, 256), 256)
        into = pl.ds(pl.multiple_of(N + i * 256, 256), 256)
        for part, ref, at, factor in ((0, qs, rows, SCALE), (1, ks, into, None), (2, vs, into, None)):
            cols = pl.ds(part * D, D)
            value = acc[rows, cols] + jnp.dot(nrm[rows, others], wqo[:, cols], preferred_element_type=F32)
            if factor is not None:
                value = value * factor
            ref[at, :] = value.astype(BF16)
        return 0

    lax.fori_loop(0, 2, second_half, 0)
    outs = []

    def put(src, dst, start, rows, i):
        span = pl.ds(start, rows)
        copy = pltpu.make_async_copy(src.at[span], dst.at[span], local.at[i])
        copy.start()
        outs.append(copy)

    put(qs, q_out, 0, N, 2)
    put(ks, k_out, N, N, 3)
    put(vs, v_out, N, N, 4)

    near_at = (1 - h) * (2 * N)
    far_at = h * (2 * N)

    def keyvals(src, first, base, slot):
        for j in range(4):
            rows = src[pl.ds(128 * (first + 2 * (j // 2)) + 64 * (j % 2), 64), :]
            nrm2[pl.ds(64 * j, 64), :] = normalize(rows, gain)
        for part, ref, out, sem in ((1, ks, k_out, slot), (2, vs, v_out, slot + 2)):
            cols = pl.ds(part * D, D)
            value = jnp.dot(nrm2[:, mine], wq[:, cols], preferred_element_type=F32)
            value = value + jnp.dot(nrm2[:, others], wqo[:, cols], preferred_element_type=F32)
            for j in range(2):
                start = pl.multiple_of(base + 128 * (first + 2 * j), 128)
                ref[pl.ds(start, 128), :] = value[128 * j : 128 * j + 128].astype(BF16)
                put(ref, out, start, 128, sem + j)

    halo(4).wait_recv()
    halo(8).start()
    halo(6).wait_recv()
    halo(9).start()
    keyvals(near, 0, near_at, 5)
    small.arrived(3)
    small.go(5, 6)
    small.arrived(2)
    small.go(7, 8)
    halo(5).wait_recv()
    halo(10).start()
    halo(7).wait_recv()
    halo(11).start()
    keyvals(near, 1, near_at, 9)
    small.arrived(5, 7)
    small.go(9)
    halo(8).wait_recv()
    halo(9).wait_recv()
    keyvals(far, 0, far_at, 13)
    small.arrived(4, 6, 8, 9)
    wo_done = pltpu.make_async_copy(woo, wo_out, local.at[21])
    wo_done.start()
    halo(10).wait_recv()
    halo(11).wait_recv()
    keyvals(far, 1, far_at, 17)
    for copy in outs:
        copy.wait()
    wo_done.wait()
    big.sent()
    small.sent()
    for i in range(12):
        halo(i).wait_send()


def gather(tokens, gain, w_qkv, w_out):
    any_ = pl.BlockSpec(memory_space=pltpu.HBM)
    vm = pl.BlockSpec(memory_space=pltpu.VMEM)
    dma = pltpu.SemaphoreType.DMA
    return pl.pallas_call(
        gather_kernel,
        name="gather",
        out_shape=(
            jax.ShapeDtypeStruct((N, D), BF16),
            jax.ShapeDtypeStruct((3 * N, D), BF16),
            jax.ShapeDtypeStruct((3 * N, D), BF16),
            jax.ShapeDtypeStruct((HALF, D), BF16),
        ),
        in_specs=[any_, vm, any_, any_],
        out_specs=(any_,) * 4,
        scratch_shapes=[
            pltpu.VMEM((N, D), BF16),
            pltpu.VMEM((HALF, 3 * D), BF16),
            pltpu.VMEM((HALF, 3 * D), BF16),
            pltpu.VMEM((HALF, D), BF16),
            pltpu.VMEM((N, D), BF16),
            pltpu.VMEM((N, D), BF16),
            pltpu.VMEM((256, D), BF16),
            pltpu.VMEM((256, D), BF16),
            pltpu.VMEM((N, D), BF16),
            pltpu.VMEM((256, D), BF16),
            pltpu.VMEM((N, 3 * D), F32),
            pltpu.VMEM((N, D), BF16),
            pltpu.VMEM((3 * N, D), BF16),
            pltpu.VMEM((3 * N, D), BF16),
            dma((10,)),
            dma((10,)),
            dma((10,)),
            dma((10,)),
            dma((12,)),
            dma((12,)),
            dma((22,)),
        ],
        compiler_params=pltpu.CompilerParams(
            collective_id=0, has_side_effects=True, vmem_limit_bytes=VMEM_LIMIT
        ),
    )(tokens, gain, w_qkv, w_out)


def attend_kernel(
    lens_ref, q_hbm, k_hbm, v_hbm, tok_hbm, wa_hbm, wb_hbm,
    hid_hbm, part_ref,
    q, k, v, tok, wa, wb, ctx, bias, hid, qid, kid, sems,
):
    sx, sy, d = lax.axis_index("sx"), lax.axis_index("sy"), lax.axis_index("dp")
    copies = [
        pltpu.make_async_copy(a, b, sems.at[i])
        for i, (a, b) in enumerate(
            ((q_hbm, q), (k_hbm, k), (v_hbm, v), (tok_hbm, tok), (wa_hbm, wa), (wb_hbm, wb))
        )
    ]
    for copy in copies:
        copy.start()
    first = (sx * 8 + sy) * N
    base = first - N

    lens = lens_ref[...].astype(F32)
    down = lax.broadcasted_iota(jnp.int32, (IMAGES, IMAGES), 0)
    along = lax.broadcasted_iota(jnp.int32, (IMAGES, IMAGES), 1)
    wide = jnp.broadcast_to(lens, (IMAGES, IMAGES))
    off_col = jnp.sum(jnp.where(along < down, wide, 0.0), axis=1, keepdims=True)
    len_col = jnp.sum(jnp.where(along == down, wide, 0.0), axis=1, keepdims=True)
    off_row = jnp.sum(
        jnp.where(down < along, jnp.broadcast_to(len_col, (IMAGES, IMAGES)), 0.0), axis=0, keepdims=True
    )
    for j in range(3):
        pos = (lax.broadcasted_iota(jnp.int32, (1, N), 1) + (base + j * N)).astype(F32)
        count = jnp.sum(jnp.where(off_col <= pos, 1.0, 0.0), axis=0, keepdims=True) - 1.0
        kid[:, pl.ds(j * N, N)] = jnp.where(pos < TOTAL, count, -1.0)
    for j in range(4):
        pos = (lax.broadcasted_iota(jnp.int32, (128, 1), 0) + (first + j * 128)).astype(F32)
        qid[pl.ds(j * 128, 128), :] = jnp.sum(jnp.where(off_row <= pos, 1.0, 0.0), axis=1, keepdims=True) - 1.0

    for copy in copies[:3]:
        copy.wait()

    def block(i, _):
        rows = pl.ds(pl.multiple_of(i * 128, 128), 128)
        begin = (first + i * 128).astype(F32)
        low = jnp.max(jnp.where(off_row <= begin, off_row, 0.0)).astype(jnp.int32)
        high = jnp.min(jnp.where(off_row > begin + 127.0, off_row, float(TOTAL))).astype(jnp.int32)
        low = (low - base) >> 7
        high = (high - base + 127) >> 7
        blocks = high - low
        ids = qid[rows, :]
        before = 0
        for size in CLASSES:
            n = size * 128

            @pl.when((blocks > before) & (blocks <= size))
            def _():
                start = pl.multiple_of(jnp.minimum(low, 12 - size) * 128, 128)
                keys = pl.ds(start, n)
                bias[:, pl.ds(0, n)] = jnp.where(ids == kid[:, keys], 0.0, -1e30)

                def two_pairs(pp, _):
                    for sub in range(2):
                        pair = pp * 2 + sub
                        tile = (pair * 5) >> 2
                        lanes = pl.ds(pl.multiple_of(tile * 128, 128), 256)
                        shift = pair * 160 - tile * 128
                        lane = lax.broadcasted_iota(jnp.int32, (1, 256), 1) - shift
                        one = (lane >= 0) & (lane < SIZE)
                        two = (lane >= SIZE) & (lane < 2 * SIZE)
                        window = q[rows, lanes]
                        both = jnp.concatenate(
                            [
                                window * jnp.where(one, 1.0, 0.0).astype(BF16),
                                window * jnp.where(two, 1.0, 0.0).astype(BF16),
                            ],
                            axis=0,
                        )
                        scores = lax.dot_general(
                            both, k[keys, lanes], (((1,), (1,)), ((), ())), preferred_element_type=F32
                        )
                        extra = bias[:, pl.ds(0, n)]
                        scores = scores + jnp.concatenate([extra, extra], axis=0)
                        top = jnp.max(scores, axis=1, keepdims=True)
                        weights = jnp.exp2(scores - top)
                        total = jnp.sum(weights, axis=1, keepdims=True)
                        mixed = jnp.dot(weights.astype(BF16), v[keys, lanes], preferred_element_type=F32)
                        mixed = mixed * (1.0 / total)
                        old = ctx[rows, lanes].astype(F32)
                        ctx[rows, lanes] = jnp.where(one, mixed[:128], jnp.where(two, mixed[128:], old)).astype(BF16)
                    return 0

                lax.fori_loop(0, 4, two_pairs, 0)

            before = size
        return 0

    lax.fori_loop(0, 4, block, 0)
    for copy in copies[3:]:
        copy.wait()
    mine = pl.ds(pl.multiple_of(d * HALF, 128), HALF)
    others = pl.ds(pl.multiple_of((1 - d) * HALF, 128), HALF)

    def project(i, _):
        rows = pl.ds(pl.multiple_of(i * 256, 256), 256)
        mixed = jnp.dot(ctx[rows, mine], wa[...], preferred_element_type=F32)
        mixed = mixed + jnp.dot(ctx[rows, others], wb[...], preferred_element_type=F32)
        hid[rows, :] = (tok[rows, :].astype(F32) + mixed).astype(BF16)
        return 0

    lax.fori_loop(0, 2, project, 0)
    out = pltpu.make_async_copy(hid, hid_hbm, sems.at[6])
    out.start()
    image = lax.broadcasted_iota(jnp.int32, (IMAGES, 1), 0).astype(F32)
    onehot = jnp.where(image == kid[:, pl.ds(N, N)], 1.0, 0.0).astype(BF16)
    sums = jnp.dot(onehot, hid[...], preferred_element_type=F32)
    part_ref[...] = (sums / len_col).astype(BF16)
    out.wait()


def attend(lengths, q, k, v, tokens, w_own, w_other):
    any_ = pl.BlockSpec(memory_space=pltpu.HBM)
    vm = pl.BlockSpec(memory_space=pltpu.VMEM)
    return pl.pallas_call(
        attend_kernel,
        name="attend",
        out_shape=(
            jax.ShapeDtypeStruct((N, D), BF16),
            jax.ShapeDtypeStruct((IMAGES, D), BF16),
        ),
        in_specs=[vm] + [any_] * 6,
        out_specs=(any_, vm),
        scratch_shapes=[
            pltpu.VMEM((N, D), BF16),
            pltpu.VMEM((3 * N, D), BF16),
            pltpu.VMEM((3 * N, D), BF16),
            pltpu.VMEM((N, D), BF16),
            pltpu.VMEM((HALF, D), BF16),
            pltpu.VMEM((HALF, D), BF16),
            pltpu.VMEM((N, D), BF16),
            pltpu.VMEM((128, 128 * CLASSES[-1]), F32),
            pltpu.VMEM((N, D), BF16),
            pltpu.VMEM((N, 1), F32),
            pltpu.VMEM((1, 3 * N), F32),
            pltpu.SemaphoreType.DMA((7,)),
        ],
        compiler_params=pltpu.CompilerParams(vmem_limit_bytes=VMEM_LIMIT),
    )(lengths, q, k, v, tokens, w_own, w_other)


def combine_kernel(
    part, out, rc, one, rx, two, ry, three, four, last,
    c_send, c_recv, x_send, x_recv, y_send, y_recv, g_send, g_recv, w_send, w_recv,
):
    sx, sy, d = lax.axis_index("sx"), lax.axis_index("sy"), lax.axis_index("dp")
    core = lax.rem(sx, 2)
    chip = sx // 2
    mate = (sx + 1 - 2 * core, sy, d)
    chips = [(lax.rem(sx + 2 * j, 8), sy, d) for j in (1, 2, 3)]
    plane = [(sx, lax.rem(sy + j, 8), d) for j in range(1, 8)]
    barrier = pltpu.get_barrier_semaphore()
    for who in [mate] + chips + plane:
        pl.semaphore_signal(barrier, inc=1, device_id=who, device_id_type=MESH)
    pl.semaphore_wait(barrier, 11)

    def remote(src, dst, send, recv, who):
        return pltpu.make_async_remote_copy(
            src_ref=src, dst_ref=dst, send_sem=send, recv_sem=recv, device_id=who, device_id_type=MESH
        )

    my_half = pl.ds(pl.multiple_of(core * 128, 128), 128)
    its_half = pl.ds(pl.multiple_of((1 - core) * 128, 128), 128)
    c_copy = remote(part.at[its_half], rc, c_send.at[0], c_recv.at[0], mate)
    c_copy.start()
    c_copy.wait_recv()
    one[...] = (part[my_half, :].astype(F32) + rc[...].astype(F32)).astype(BF16)

    def strip(owner):
        return pl.ds(pl.multiple_of(owner * 32, 32), 32)

    x_copies = [
        remote(one.at[strip(lax.rem(chip + j, 4))], rx.at[j - 1], x_send.at[j - 1], x_recv.at[j - 1], chips[j - 1])
        for j in (1, 2, 3)
    ]
    for copy in x_copies:
        copy.start()
    for copy in x_copies:
        copy.wait_recv()
    total = one[strip(chip), :].astype(F32)
    for j in range(3):
        total = total + rx[j].astype(F32)
    for j in range(2):
        two[j] = total[:, j * HALF : (j + 1) * HALF]

    def spot(owner):
        return pl.ds(pl.multiple_of((owner // 2) * 8, 8), 8)

    y_copies = []
    for j in range(1, 8):
        to = lax.rem(sy + j, 8)
        y_copies.append(
            remote(two.at[lax.rem(to, 2), spot(to)], ry.at[j - 1], y_send.at[j - 1], y_recv.at[j - 1], plane[j - 1])
        )
    for copy in y_copies:
        copy.start()
    for copy in y_copies:
        copy.wait_recv()
    side = lax.rem(sy, 2)
    total = two[side, spot(sy), :]
    for j in range(7):
        total = total + ry[j]
    three[side, spot(sy), :] = total
    g_copies = [
        remote(three.at[side, spot(sy)], three.at[side, spot(sy)], g_send.at[j], g_recv.at[j], plane[j])
        for j in range(7)
    ]
    for copy in g_copies:
        copy.start()
    for copy in g_copies:
        copy.wait_recv()
    four[strip(chip), :] = jnp.concatenate([three[0], three[1]], axis=1).astype(BF16)
    w_copies = [
        remote(four.at[strip(chip)], four.at[strip(chip)], w_send.at[j], w_recv.at[j], chips[j]) for j in range(3)
    ]
    for copy in w_copies:
        copy.start()
    for copy in w_copies:
        copy.wait_recv()
    l_copy = remote(four, last, c_send.at[1], c_recv.at[1], mate)
    l_copy.start()
    out[my_half, :] = four[...]
    l_copy.wait_recv()
    out[its_half, :] = last[...]
    for copy in [c_copy, l_copy] + x_copies + y_copies + g_copies + w_copies:
        copy.wait_send()


def combine(part):
    vm = pl.BlockSpec(memory_space=pltpu.VMEM)
    dma = pltpu.SemaphoreType.DMA
    return pl.pallas_call(
        combine_kernel,
        name="combine",
        out_shape=jax.ShapeDtypeStruct((IMAGES, D), BF16),
        in_specs=[vm],
        out_specs=vm,
        scratch_shapes=[
            pltpu.VMEM((128, D), BF16),
            pltpu.VMEM((128, D), BF16),
            pltpu.VMEM((3, 32, D), BF16),
            pltpu.VMEM((2, 32, HALF), F32),
            pltpu.VMEM((7, 8, HALF), F32),
            pltpu.VMEM((2, 32, HALF), F32),
            pltpu.VMEM((128, D), BF16),
            pltpu.VMEM((128, D), BF16),
            dma((2,)),
            dma((2,)),
            dma((3,)),
            dma((3,)),
            dma((7,)),
            dma((7,)),
            dma((7,)),
            dma((7,)),
            dma((3,)),
            dma((3,)),
        ],
        compiler_params=pltpu.CompilerParams(collective_id=1, has_side_effects=True),
    )(part)


def shards(tokens, lengths, ln_gain, w_qkv, w_out):
    rows = tokens.reshape(N, D)
    q, k, v, w_other = gather(rows, ln_gain.reshape(1, D), w_qkv, w_out)
    hidden, part = attend(lengths, q, k, v, rows, w_out, w_other)
    pooled = combine(part).astype(F32)
    return hidden.reshape(1, N, D), pooled.reshape(1, IMAGES, D)


def solution(mesh):
    in_specs = (P("dp", ("sx", "sy"), None), P("dp", None), P(), P("dp", None), P("dp", None))
    out_specs = (P("dp", ("sx", "sy"), None), P("dp", None, None))
    return jax.shard_map(shards, mesh=mesh, in_specs=in_specs, out_specs=out_specs, check_vma=False)
```

time: 482 us -> 141 us (0.29)
  waiting for transfers between devices: 248 us -> 0 us
  Pallas kernels: 0 us -> 138 us
  matrix products: 72.2 us -> 0 us
  blocking collectives: 57.2 us -> 0 us
  loops' own time: 31.3 us -> 0 us
  local copies, waits for them, and re-layouts: 30.5 us -> 1.29 us
  starting transfers between devices: 20.6 us -> 0 us
  other arithmetic: 19.6 us -> 2.23 us
    all_to_all x1 -> x0, waiting for transfers between devices: 142 us -> none  [from_everyone(): lax.all_to_all(jnp.broadcast_to(shard[None], (length, *shard.shape)), axi...]
    pallas_call x0 -> x3, Pallas kernels: none -> 138 us  [the longest x1 79 us: gather(): pl.pallas_call(gather_kernel, name='gather', out_shape=(jax.ShapeDtypeStr...]
    ppermute x2 -> x0, waiting for transfers between devices: 106 us -> none  [the longest x1 78.1 us: with_halo(): lax.ppermute(initial, axis, [(b, a) for a, b in up])]
    dot_general x35 -> x0, matrix products: 72.2 us -> none  [the longest x16 28.8 us: one_head(): jnp.dot(probs, v_head, preferred_element_type=jnp.float32)]
    all_to_all x2 -> x0, blocking collectives: 57.2 us -> none  [the longest x1 31.1 us: sent_and_summed(): lax.all_to_all(pieces, axis, split_axis=0, concat_axis=0, tiled=True)]
    another operation x1 -> x0, loops' own time: 31.3 us -> none  [one_block(): outcome = lax.map(one_head, jnp.arange(heads, dtype=jnp.int32))]
    ppermute x2 -> x0, starting transfers between devices: 11.9 us -> none  [the longest x1 10 us: with_halo(): lax.ppermute(initial, axis, [(b, a) for a, b in up])]
    reduce_sum x21 -> x0, other arithmetic: 10.8 us -> none  [the longest x16 9.16 us: one_head(): jnp.sum(weights, axis=1, keepdims=True)]
  transfers between devices with their start and end apart: 3 -> 0, of which waited for: 3 -> 0; matrix products, arithmetic and copies ran while one was open for 1% -> 0% of each run, Pallas kernels for 0% -> 0%
where the time goes in v1:
time: 141 us; the launch traced here: 143 us
  Pallas kernels  138 us (98%)
  other arithmetic  2.23 us (2%)
    pallas_call x1, Pallas kernels, gather(): pl.pallas_call(gather_kernel, name='gather', out_shape=(jax.ShapeDtypeStr...  79 us
    pallas_call x1, Pallas kernels, combine(): pl.pallas_call(combine_kernel, name='combine', out_shape=jax.ShapeDtypeSt...  38.1 us
    pallas_call x1, Pallas kernels, attend(): pl.pallas_call(attend_kernel, name='attend', out_shape=(jax.ShapeDtypeStr...  21.3 us

profile of v1, /device:TPU:1, one launch (start us, length us, event | category | flops | bytes accessed | tf_op | source)
XLA Modules:
  0.0 142.6 jit_solution(17014173119047162208)
XLA Ops:
  0.6 1.3 reshape.20.gain_ref
  1.9 79.0 %gather.1 = (bf16[512,1280]{1,0:T(8,128)(2,1)}, bf16[1536,1280]{1,0:T(8,128)(2,1)}, bf16[1536,1280]{1,0:T(8,128)(2,1)}, bf16[640,1280]{1,0:T(8,128)(2,1)}) custom-call(bf16[512,1280]{1,0:T(8,128)(2,1)} %bitcast.5, f32[1,1280]{1,0:T(1,128)} %reshape.20.gain_ref, bf16[640,3840]{1,0:T(8,128)(2,1)} %wq_hbm.1, bf16[640,1280]{1,0:T(8,128)(2,1)} %wa_hbm.1), custom_call_target="tpu_custom_call" | custom-call | tf_op jit(solution)/shard_map/gather/pallas_call | solution.py:276
  81.0 21.3 %attend.1 = (bf16[512,1280]{1,0:T(8,128)(2,1)}, bf16[256,1280]{1,0:T(8,128)(2,1)}) custom-call(s32[1,256]{1,0:T(1,128)} %lens_ref.1, bf16[512,1280]{1,0:T(8,128)(2,1)} %get-tuple-element.8.q_hbm, bf16[1536,1280]{1,0:T(8,128)(2,1)} %get-tuple-element.9.k_hbm, bf16[1536,1280]{1,0:T(8,128)(2,1)} %get-tuple-element.10.v_hbm, bf16[512,1280]{1,0:T(8,128)(2,1)} %bitcast.6, ...), custom_call_target="tpu_custom_call" | custom-call | tf_op jit(solution)/shard_map/attend/pallas_call | solution.py:434
  102.3 38.1 %combine.1 = bf16[256,1280]{1,0:T(8,128)(2,1)} custom-call(bf16[256,1280]{1,0:T(8,128)(2,1)} %get-tuple-element.13.part), custom_call_target="tpu_custom_call" | custom-call | tf_op jit(solution)/shard_map/combine/pallas_call | solution.py:551
  140.3 2.2 %bitcast_convert_fusion = f32[1,256,1280]{2,1,0:T(8,128)} fusion(bf16[256,1280]{1,0:T(8,128)(2,1)} %combine.1), kind=kLoop, calls=%fused_computation | loop fusion | flops 327680 | bytes 1966080 | tf_op jit(solution)/shard_map/reshape | solution.py:586

commit v2 on v1

--- a/solution.py
+++ b/solution.py
@@ -18,6 +18,7 @@
 TOTAL = 32768
 SCALE = SIZE**-0.5 * math.log2(math.e)
 PIECE = 80
+UPPER = (0, 1, 2, 6)
 CLASSES = (2, 3, 4, 5, 6, 9)
 VMEM_LIMIT = 62 * 1024 * 1024
 
@@ -50,61 +51,112 @@
 
 
 class Exchange:
-    def __init__(self, own, other, width, sx, mate, where, send, recv):
-        self.own, self.other, self.width = own, other, width
-        self.sx, self.mate, self.where = sx, mate, where
+    def __init__(self, refs, sx, where, send, recv):
+        self.refs, self.sx, self.where = refs, sx, where
         self.send, self.recv = send, recv
-        self.started = []
-
-    def rows(self, owner):
-        return pl.ds(pl.multiple_of(lax.rem(owner + 8, 8) * PIECE, 16), PIECE)
-
-    def copy(self, i, src, owner, cols, to):
-        rows = self.rows(owner)
+
+    def copy(self, kind, c):
+        own, other = self.refs[c // 6]
+        cols = pl.ds((c % 6) * HALF, HALF)
+        upper = c in UPPER
+        ahead, src, to = (
+            (0, own, "a" if upper else "b"),
+            (0, other, "xp"),
+            (0, other, "xm"),
+            (0, other, "core"),
+            (2, other, "xm") if upper else (6, other, "xp"),
+            (2, other, "core"),
+            (6, other, "core"),
+            (4, other, "core"),
+        )[kind]
+        rows = pl.ds(pl.multiple_of(lax.rem(self.sx + ahead, 8) * PIECE, 16), PIECE)
         return pltpu.make_async_remote_copy(
             src_ref=src.at[rows, cols],
-            dst_ref=self.other.at[rows, cols],
-            send_sem=self.send.at[i],
-            recv_sem=self.recv.at[i],
+            dst_ref=other.at[rows, cols],
+            send_sem=self.send.at[kind * 8 + c],
+            recv_sem=self.recv.at[kind * 8 + c],
             device_id=self.where[to],
             device_id_type=MESH,
         )
 
-    def describe(self, i):
-        sx, w = self.sx, self.width
-        low, high, full = pl.ds(0, w // 2), pl.ds(w // 2, w // 2), pl.ds(0, w)
-        table = (
-            (self.own, sx, low, "a"),
-            (self.own, sx, high, "b"),
-            (self.other, sx, full, "xp"),
-            (self.other, sx, full, "xm"),
-            (self.other, sx, full, "core"),
-            (self.other, sx + 2, low, "xm"),
-            (self.other, sx + 2, full, "core"),
-            (self.other, sx - 2, high, "xp"),
-            (self.other, sx - 2, full, "core"),
-            (self.other, sx + 4, full, "core"),
+    def step(self, cs, waits, goes):
+        for c in cs:
+            for kind in waits:
+                self.copy(kind, c).wait_recv()
+            for kind in goes:
+                self.copy(kind, c).start()
+
+    def begin(self, *cs):
+        self.step(cs, (), (0,))
+
+    def from_y(self, *cs):
+        self.step(cs, (0,), (1, 2, 3))
+
+    def from_x(self, *cs):
+        self.step(cs, (1, 2), (4, 5, 6))
+
+    def from_far(self, *cs):
+        self.step(cs, (4,), (7,))
+
+    def finish(self, *cs):
+        self.step(cs, (3, 5, 6, 7), ())
+
+    def sent(self):
+        for c in range(8):
+            for kind in range(8):
+                self.copy(kind, c).wait_send()
+
+
+class Halo:
+    def __init__(self, tok, ta, tb, near, far, where, send, recv):
+        self.table = []
+        for i in range(4):
+            self.table += [(tok, i, ta, i, "a"), (tok, 4 + i, tb, i, "b")]
+        for i in range(4):
+            self.table += [(ta, i, near, i, "b"), (tb, i, near, 4 + i, "a")]
+        for i in range(4):
+            self.table += [(near, i, far, i, "z"), (near, 4 + i, far, 4 + i, "z")]
+        self.where, self.send, self.recv = where, send, recv
+
+    def copy(self, i):
+        src, at, dst, to, name = self.table[i]
+        return pltpu.make_async_remote_copy(
+            src_ref=src.at[pl.ds(64 * at, 64)],
+            dst_ref=dst.at[pl.ds(64 * to, 64)],
+            send_sem=self.send.at[i],
+            recv_sem=self.recv.at[i],
+            device_id=self.where[name],
+            device_id_type=MESH,
         )
-        return self.copy(i, *table[i])
-
-    def go(self, *which):
-        for i in which:
-            self.describe(i).start()
-
-    def arrived(self, *which):
-        for i in which:
-            self.describe(i).wait_recv()
+
+    def own(self, i):
+        self.copy(2 * i).start()
+        self.copy(2 * i + 1).start()
+
+    def relay(self, i):
+        for j in (2 * i, 2 * i + 1):
+            self.copy(j).wait_recv()
+            self.copy(8 + j).start()
+
+    def onward(self, i):
+        for j in (2 * i, 2 * i + 1):
+            self.copy(8 + j).wait_recv()
+            self.copy(16 + j).start()
+
+    def arrived(self, i):
+        for j in (2 * i, 2 * i + 1):
+            self.copy(16 + j).wait_recv()
 
     def sent(self):
-        for i in range(10):
-            self.describe(i).wait_send()
+        for i in range(24):
+            self.copy(i).wait_send()
 
 
 def gather_kernel(
     tok_hbm, gain_ref, wq_hbm, wo_hbm,
     q_out, k_out, v_out, wo_out,
     tok, wq, wqo, woo, near, far, ta, tb, nrm, nrm2, acc, qs, ks, vs,
-    wq_send, wq_recv, wo_send, wo_recv, h_send, h_recv, local,
+    w_send, w_recv, h_send, h_recv, local,
 ):
     sx, sy, d, h, mate, where = places()
     barrier = pltpu.get_barrier_semaphore()
@@ -117,83 +169,34 @@
     wq_in.start()
     pl.semaphore_wait(barrier, 7)
 
-    big = Exchange(wq_hbm, wqo, 3 * D, sx, mate, where, wq_send, wq_recv)
-    small = Exchange(wo_hbm, woo, D, sx, mate, where, wo_send, wo_recv)
-
-    def chunk(i):
-        return pl.ds(128 * i, 128)
-
-    table = (
-        (tok_hbm, 0, ta, 0, "a"),
-        (tok_hbm, 1, ta, 1, "a"),
-        (tok_hbm, 2, tb, 0, "b"),
-        (tok_hbm, 3, tb, 1, "b"),
-        (ta, 0, near, 0, "b"),
-        (ta, 1, near, 1, "b"),
-        (tb, 0, near, 2, "a"),
-        (tb, 1, near, 3, "a"),
-        (near, 0, far, 0, "z"),
-        (near, 2, far, 2, "z"),
-        (near, 1, far, 1, "z"),
-        (near, 3, far, 3, "z"),
-    )
-
-    def halo(i):
-        src, at, dst, to, name = table[i]
-        return pltpu.make_async_remote_copy(
-            src_ref=src.at[chunk(at)],
-            dst_ref=dst.at[chunk(to)],
-            send_sem=h_send.at[i],
-            recv_sem=h_recv.at[i],
-            device_id=where[name],
-            device_id_type=MESH,
-        )
-
-    big.go(0, 1)
-    for i in (0, 2, 1, 3):
-        halo(i).start()
-    small.go(0, 1)
-
-    gain = gain_ref[...]
+    weights = Exchange(((wq_hbm, wqo), (wo_hbm, woo)), sx, where, w_send, w_recv)
+    halo = Halo(tok_hbm, ta, tb, near, far, where, h_send, h_recv)
+    gain = gain_ref[...].reshape(1, D)
     mine = pl.ds(pl.multiple_of(d * HALF, 128), HALF)
     others = pl.ds(pl.multiple_of((1 - d) * HALF, 128), HALF)
-
-    tok_in.wait()
+    near_at = (1 - h) * (2 * N)
+    far_at = h * (2 * N)
+    outs = []
+
+    def put(src, dst, start, rows, i):
+        span = pl.ds(start, rows)
+        copy = pltpu.make_async_copy(src.at[span], dst.at[span], local.at[i])
+        copy.start()
+        outs.append(copy)
 
     def norm_own(i, _):
         rows = pl.ds(pl.multiple_of(i * 64, 64), 64)
         nrm[rows, :] = normalize(tok[rows, :], gain)
         return 0
 
-    lax.fori_loop(0, N // 64, norm_own, 0)
-    wq_in.wait()
-
-    def first_half(i, _):
-        rows = pl.ds(pl.multiple_of(i * 256, 256), 256)
-        for part in range(3):
+    def first_half(part):
+        def one(i, _):
+            rows = pl.ds(pl.multiple_of(i * 256, 256), 256)
             cols = pl.ds(part * D, D)
             acc[rows, cols] = jnp.dot(nrm[rows, mine], wq[:, cols], preferred_element_type=F32)
-        return 0
-
-    lax.fori_loop(0, 2, first_half, 0)
-
-    big.arrived(0, 1)
-    big.go(2, 3, 4)
-    for i, j in ((0, 4), (2, 6)):
-        halo(i).wait_recv()
-        halo(j).start()
-    big.arrived(3)
-    big.go(5, 6)
-    big.arrived(2)
-    big.go(7, 8)
-    for i, j in ((1, 5), (3, 7)):
-        halo(i).wait_recv()
-        halo(j).start()
-    small.arrived(0, 1)
-    small.go(2, 3, 4)
-    big.arrived(5, 7)
-    big.go(9)
-    big.arrived(4, 6, 8, 9)
+            return 0
+
+        lax.fori_loop(0, 2, one, 0)
 
     def second_half(i, _):
         rows = pl.ds(pl.multiple_of(i * 256, 256), 256)
@@ -205,22 +208,6 @@
                 value = value * factor
             ref[at, :] = value.astype(BF16)
         return 0
-
-    lax.fori_loop(0, 2, second_half, 0)
-    outs = []
-
-    def put(src, dst, start, rows, i):
-        span = pl.ds(start, rows)
-        copy = pltpu.make_async_copy(src.at[span], dst.at[span], local.at[i])
-        copy.start()
-        outs.append(copy)
-
-    put(qs, q_out, 0, N, 2)
-    put(ks, k_out, N, N, 3)
-    put(vs, v_out, N, N, 4)
-
-    near_at = (1 - h) * (2 * N)
-    far_at = h * (2 * N)
 
     def keyvals(src, first, base, slot):
         for j in range(4):
@@ -235,38 +222,67 @@
                 ref[pl.ds(start, 128), :] = value[128 * j : 128 * j + 128].astype(BF16)
                 put(ref, out, start, 128, sem + j)
 
-    halo(4).wait_recv()
-    halo(8).start()
-    halo(6).wait_recv()
-    halo(9).start()
-    keyvals(near, 0, near_at, 5)
-    small.arrived(3)
-    small.go(5, 6)
-    small.arrived(2)
-    small.go(7, 8)
-    halo(5).wait_recv()
-    halo(10).start()
-    halo(7).wait_recv()
-    halo(11).start()
-    keyvals(near, 1, near_at, 9)
-    small.arrived(5, 7)
-    small.go(9)
-    halo(8).wait_recv()
-    halo(9).wait_recv()
-    keyvals(far, 0, far_at, 13)
-    small.arrived(4, 6, 8, 9)
-    wo_done = pltpu.make_async_copy(woo, wo_out, local.at[21])
-    wo_done.start()
-    halo(10).wait_recv()
-    halo(11).wait_recv()
-    keyvals(far, 1, far_at, 17)
-    for copy in outs:
-        copy.wait()
-    wo_done.wait()
-    big.sent()
-    small.sent()
-    for i in range(12):
-        halo(i).wait_send()
+    with jax.named_scope("g0_start"):
+        weights.begin(0, 3, 1, 4, 2, 5)
+        halo.own(0)
+        halo.own(1)
+        tok_in.wait()
+        lax.fori_loop(0, N // 64, norm_own, 0)
+        weights.from_y(0, 3)
+        wq_in.wait()
+        first_half(0)
+        weights.from_y(1, 4)
+        first_half(1)
+        weights.from_y(2, 5)
+        first_half(2)
+    with jax.named_scope("g1_relay0"):
+        halo.relay(0)
+        halo.own(2)
+        weights.from_x(0, 3, 1)
+    with jax.named_scope("g2_relay1"):
+        halo.relay(1)
+        weights.begin(6, 7)
+        halo.own(3)
+        weights.from_x(4, 2, 5)
+        halo.onward(0)
+    with jax.named_scope("g3_relay2"):
+        halo.relay(2)
+        halo.onward(1)
+        weights.from_far(0, 3, 1, 4, 2, 5)
+        halo.relay(3)
+    with jax.named_scope("g4_weights"):
+        weights.finish(0, 3, 1, 4, 2, 5)
+        weights.from_y(6, 7)
+    with jax.named_scope("g5_own"):
+        lax.fori_loop(0, 2, second_half, 0)
+        put(qs, q_out, 0, N, 2)
+        put(ks, k_out, N, N, 3)
+        put(vs, v_out, N, N, 4)
+    with jax.named_scope("g6_near2"):
+        halo.onward(2)
+        weights.from_x(6, 7)
+        keyvals(near, 0, near_at, 5)
+    with jax.named_scope("g7_near3"):
+        halo.onward(3)
+        weights.from_far(6, 7)
+        keyvals(near, 1, near_at, 9)
+    with jax.named_scope("g8_far1"):
+        halo.arrived(0)
+        halo.arrived(1)
+        keyvals(far, 0, far_at, 13)
+        weights.finish(6, 7)
+        wo_done = pltpu.make_async_copy(woo, wo_out, local.at[21])
+        wo_done.start()
+    with jax.named_scope("g9_far3"):
+        halo.arrived(2)
+        halo.arrived(3)
+    with jax.named_scope("g10_end"):
+        keyvals(far, 1, far_at, 17)
+        for copy in outs:
+            copy.wait()
+        wo_done.wait()
+        weights.sent()
+        halo.sent()
 
 
 def gather(tokens, gain, w_qkv, w_out):
@@ -299,12 +315,10 @@
             pltpu.VMEM((N, D), BF16),
             pltpu.VMEM((3 * N, D), BF16),
             pltpu.VMEM((3 * N, D), BF16),
-            dma((10,)),
-            dma((10,)),
-            dma((10,)),
-            dma((10,)),
-            dma((12,)),
-            dma((12,)),
+            dma((64,)),
+            dma((64,)),
+            dma((24,)),
+            dma((24,)),
             dma((22,)),
         ],
         compiler_params=pltpu.CompilerParams(
@@ -538,9 +552,9 @@
         copy.wait_recv()
     l_copy = remote(four, last, c_send.at[1], c_recv.at[1], mate)
     l_copy.start()
-    out[my_half, :] = four[...]
+    out[my_half, :] = four[...].astype(F32)
     l_copy.wait_recv()
-    out[its_half, :] = last[...]
+    out[its_half, :] = last[...].astype(F32)
     for copy in [c_copy, l_copy] + x_copies + y_copies + g_copies + w_copies:
         copy.wait_send()
 
@@ -551,7 +565,7 @@
     return pl.pallas_call(
         combine_kernel,
         name="combine",
-        out_shape=jax.ShapeDtypeStruct((IMAGES, D), BF16),
+        out_shape=jax.ShapeDtypeStruct((IMAGES, D), F32),
         in_specs=[vm],
         out_specs=vm,
         scratch_shapes=[
@@ -580,9 +594,9 @@
 
 def shards(tokens, lengths, ln_gain, w_qkv, w_out):
     rows = tokens.reshape(N, D)
-    q, k, v, w_other = gather(rows, ln_gain.reshape(1, D), w_qkv, w_out)
+    q, k, v, w_other = gather(rows, ln_gain, w_qkv, w_out)
     hidden, part = attend(lengths, q, k, v, rows, w_out, w_other)
-    pooled = combine(part).astype(F32)
+    pooled = combine(part)
     return hidden.reshape(1, N, D), pooled.reshape(1, IMAGES, D)
 
 

time: 141 us -> 126 us (0.89); the launches traced: 143 us -> 125 us
  Pallas kernels: 138 us -> 122 us
  other arithmetic: 2.23 us -> 0 us
    pallas_call x1, Pallas kernels: 79 us -> 66.3 us  [gather(): pl.pallas_call(gather_kernel, name='gather', out_shape=(jax.ShapeDtypeStr...]
    pallas_call x1, Pallas kernels: 38.1 us -> 33.9 us  [combine(): pl.pallas_call(combine_kernel, name='combine', out_shape=jax.ShapeDtypeSt...]
    unnamed x0 -> x1, local copies, waits for them, and re-layouts: none -> 2.46 us
    reshape x1 -> x0, other arithmetic: 2.23 us -> none  [shards(): return (hidden.reshape(1, N, D), pooled.reshape(1, IMAGES, D))]
where the time goes in v2:
time: 126 us; the launch traced here: 125 us
  Pallas kernels  122 us (97%)
  local copies, waits for them, and re-layouts  2.46 us (2%)
    pallas_call x1, Pallas kernels, gather(): pl.pallas_call(gather_kernel, name='gather', out_shape=(jax.ShapeDtypeStr...  66.3 us
    pallas_call x1, Pallas kernels, combine(): pl.pallas_call(combine_kernel, name='combine', out_shape=jax.ShapeDtypeSt...  33.9 us
    pallas_call x1, Pallas kernels, attend(): pl.pallas_call(attend_kernel, name='attend', out_shape=(jax.ShapeDtypeStr...  21.7 us

profile of v2, /device:TPU:1, one launch (start us, length us, event | category | flops | bytes accessed | tf_op | source)
XLA Modules:
  0.0 125.1 jit_solution(17126447750407664869)
XLA Ops:
  0.6 66.3 %gather.1 = (bf16[512,1280]{1,0:T(8,128)(2,1)}, bf16[1536,1280]{1,0:T(8,128)(2,1)}, bf16[1536,1280]{1,0:T(8,128)(2,1)}, bf16[640,1280]{1,0:T(8,128)(2,1)}) custom-call(bf16[512,1280]{1,0:T(8,128)(2,1)} %bitcast.4, f32[1280]{0:T(1024)} %gain_ref.1, bf16[640,3840]{1,0:T(8,128)(2,1)} %wq_hbm.1, bf16[640,1280]{1,0:T(8,128)(2,1)} %wa_hbm.1), custom_call_target="tpu_custom_call" | custom-call | tf_op jit(solution)/shard_map/gather/pallas_call | solution.py:292
  67.0 21.7 %attend.1 = (bf16[512,1280]{1,0:T(8,128)(2,1)}, bf16[256,1280]{1,0:T(8,128)(2,1)}) custom-call(s32[1,256]{1,0:T(1,128)} %lens_ref.1, bf16[512,1280]{1,0:T(8,128)(2,1)} %get-tuple-element.8.q_hbm, bf16[1536,1280]{1,0:T(8,128)(2,1)} %get-tuple-element.9.k_hbm, bf16[1536,1280]{1,0:T(8,128)(2,1)} %get-tuple-element.10.v_hbm, bf16[512,1280]{1,0:T(8,128)(2,1)} %bitcast.5, ...), custom_call_target="tpu_custom_call" | custom-call | tf_op jit(solution)/shard_map/attend/pallas_call | solution.py:448
  88.7 33.9 %combine.1 = f32[256,1280]{1,0:T(8,128)} custom-call(bf16[256,1280]{1,0:T(8,128)(2,1)} %get-tuple-element.13.part), custom_call_target="tpu_custom_call" | custom-call | tf_op jit(solution)/shard_map/combine/pallas_call | solution.py:565
  122.7 2.5 %copy.8 = f32[1,256,1280]{2,1,0:T(8,128)} copy(f32[1,256,1280]{2,1,0:T(8,128)} %bitcast.3) | data formatting | bytes 2621440

commit v3 on v2

--- a/solution.py
+++ b/solution.py
@@ -20,7 +20,7 @@
 PIECE = 80
 UPPER = (0, 1, 2, 6)
 CLASSES = (2, 3, 4, 5, 6, 9)
-VMEM_LIMIT = 62 * 1024 * 1024
+MIB = 1024 * 1024
 
 
 def places():
@@ -154,8 +154,8 @@
 
 def gather_kernel(
     tok_hbm, gain_ref, wq_hbm, wo_hbm,
-    q_out, k_out, v_out, wo_out,
-    tok, wq, wqo, woo, near, far, ta, tb, nrm, nrm2, acc, qs, ks, vs,
+    qs, ks, vs, woo,
+    tok, wq, wqo, near, far, ta, tb, nrm, nrm2, acc,
     w_send, w_recv, h_send, h_recv, local,
 ):
     sx, sy, d, h, mate, where = places()
@@ -176,13 +176,6 @@
     others = pl.ds(pl.multiple_of((1 - d) * HALF, 128), HALF)
     near_at = (1 - h) * (2 * N)
     far_at = h * (2 * N)
-    outs = []
-
-    def put(src, dst, start, rows, i):
-        span = pl.ds(start, rows)
-        copy = pltpu.make_async_copy(src.at[span], dst.at[span], local.at[i])
-        copy.start()
-        outs.append(copy)
 
     def norm_own(i, _):
         rows = pl.ds(pl.multiple_of(i * 64, 64), 64)
@@ -209,18 +202,17 @@
             ref[at, :] = value.astype(BF16)
         return 0
 
-    def keyvals(src, first, base, slot):
+    def keyvals(src, first, base):
         for j in range(4):
             rows = src[pl.ds(128 * (first + 2 * (j // 2)) + 64 * (j % 2), 64), :]
             nrm2[pl.ds(64 * j, 64), :] = normalize(rows, gain)
-        for part, ref, out, sem in ((1, ks, k_out, slot), (2, vs, v_out, slot + 2)):
+        for part, ref in ((1, ks), (2, vs)):
             cols = pl.ds(part * D, D)
             value = jnp.dot(nrm2[:, mine], wq[:, cols], preferred_element_type=F32)
             value = value + jnp.dot(nrm2[:, others], wqo[:, cols], preferred_element_type=F32)
             for j in range(2):
                 start = pl.multiple_of(base + 128 * (first + 2 * j), 128)
                 ref[pl.ds(start, 128), :] = value[128 * j : 128 * j + 128].astype(BF16)
-                put(ref, out, start, 128, sem + j)
 
     with jax.named_scope("g0_start"):
         weights.begin(0, 3, 1, 4, 2, 5)
@@ -255,34 +247,34 @@
         weights.from_y(6, 7)
     with jax.named_scope("g5_own"):
         lax.fori_loop(0, 2, second_half, 0)
-        put(qs, q_out, 0, N, 2)
-        put(ks, k_out, N, N, 3)
-        put(vs, v_out, N, N, 4)
     with jax.named_scope("g6_near2"):
         halo.onward(2)
         weights.from_x(6, 7)
-        keyvals(near, 0, near_at, 5)
+        keyvals(near, 0, near_at)
     with jax.named_scope("g7_near3"):
         halo.onward(3)
         weights.from_far(6, 7)
-        keyvals(near, 1, near_at, 9)
+        keyvals(near, 1, near_at)
     with jax.named_scope("g8_far1"):
         halo.arrived(0)
         halo.arrived(1)
-        keyvals(far, 0, far_at, 13)
+        keyvals(far, 0, far_at)
         weights.finish(6, 7)
-        wo_done = pltpu.make_async_copy(woo, wo_out, local.at[21])
-        wo_done.start()
     with jax.named_scope("g9_far3"):
         halo.arrived(2)
         halo.arrived(3)
     with jax.named_scope("g10_end"):
-        keyvals(far, 1, far_at, 17)
-        for copy in outs:
-            copy.wait()
-        wo_done.wait()
+        keyvals(far, 1, far_at)
         weights.sent()
         halo.sent()
+
+
+def held(x):
+    return pltpu.with_memory_space_constraint(x, pltpu.VMEM)
+
+
+def outside(x):
+    return pltpu.with_memory_space_constraint(x, pltpu.HBM)
 
 
 def gather(tokens, gain, w_qkv, w_out):
@@ -293,18 +285,17 @@
         gather_kernel,
         name="gather",
         out_shape=(
-            jax.ShapeDtypeStruct((N, D), BF16),
-            jax.ShapeDtypeStruct((3 * N, D), BF16),
-            jax.ShapeDtypeStruct((3 * N, D), BF16),
-            jax.ShapeDtypeStruct((HALF, D), BF16),
+            pltpu.VMEM((N, D), BF16),
+            pltpu.VMEM((3 * N, D), BF16),
+            pltpu.VMEM((3 * N, D), BF16),
+            pltpu.VMEM((HALF, D), BF16),
         ),
         in_specs=[any_, vm, any_, any_],
-        out_specs=(any_,) * 4,
+        out_specs=(vm,) * 4,
         scratch_shapes=[
             pltpu.VMEM((N, D), BF16),
             pltpu.VMEM((HALF, 3 * D), BF16),
             pltpu.VMEM((HALF, 3 * D), BF16),
-            pltpu.VMEM((HALF, D), BF16),
             pltpu.VMEM((N, D), BF16),
             pltpu.VMEM((N, D), BF16),
             pltpu.VMEM((256, D), BF16),
@@ -312,31 +303,28 @@
             pltpu.VMEM((N, D), BF16),
             pltpu.VMEM((256, D), BF16),
             pltpu.VMEM((N, 3 * D), F32),
-            pltpu.VMEM((N, D), BF16),
-            pltpu.VMEM((3 * N, D), BF16),
-            pltpu.VMEM((3 * N, D), BF16),
             dma((64,)),
             dma((64,)),
             dma((24,)),
             dma((24,)),
-            dma((22,)),
+            dma((2,)),
         ],
         compiler_params=pltpu.CompilerParams(
-            collective_id=0, has_side_effects=True, vmem_limit_bytes=VMEM_LIMIT
+            collective_id=0, has_side_effects=True, vmem_limit_bytes=40 * MIB
         ),
-    )(tokens, gain, w_qkv, w_out)
+    )(outside(tokens), gain, outside(w_qkv), outside(w_out))
 
 
 def attend_kernel(
-    lens_ref, q_hbm, k_hbm, v_hbm, tok_hbm, wa_hbm, wb_hbm,
+    lens_ref, q, k, v, wb, tok_hbm, wa_hbm,
     hid_hbm, part_ref,
-    q, k, v, tok, wa, wb, ctx, bias, hid, qid, kid, sems,
+    tok, wa, ctx, bias, hid, qid, kid, sems,
 ):
     sx, sy, d = lax.axis_index("sx"), lax.axis_index("sy"), lax.axis_index("dp")
     copies = [
         pltpu.make_async_copy(a, b, sems.at[i])
         for i, (a, b) in enumerate(
-            ((q_hbm, q), (k_hbm, k), (v_hbm, v), (tok_hbm, tok), (wa_hbm, wa), (wb_hbm, wb))
+            ((tok_hbm, tok), (wa_hbm, wa))
         )
     ]
     for copy in copies:
@@ -360,9 +348,6 @@
     for j in range(4):
         pos = (lax.broadcasted_iota(jnp.int32, (128, 1), 0) + (first + j * 128)).astype(F32)
         qid[pl.ds(j * 128, 128), :] = jnp.sum(jnp.where(off_row <= pos, 1.0, 0.0), axis=1, keepdims=True) - 1.0
-
-    for copy in copies[:3]:
-        copy.wait()
 
     def block(i, _):
         rows = pl.ds(pl.multiple_of(i * 128, 128), 128)
@@ -420,7 +405,7 @@
         return 0
 
     lax.fori_loop(0, 4, block, 0)
-    for copy in copies[3:]:
+    for copy in copies:
         copy.wait()
     mine = pl.ds(pl.multiple_of(d * HALF, 128), HALF)
     others = pl.ds(pl.multiple_of((1 - d) * HALF, 128), HALF)
@@ -433,7 +418,7 @@
         return 0
 
     lax.fori_loop(0, 2, project, 0)
-    out = pltpu.make_async_copy(hid, hid_hbm, sems.at[6])
+    out = pltpu.make_async_copy(hid, hid_hbm, sems.at[2])
     out.start()
     image = lax.broadcasted_iota(jnp.int32, (IMAGES, 1), 0).astype(F32)
     onehot = jnp.where(image == kid[:, pl.ds(N, N)], 1.0, 0.0).astype(BF16)
@@ -442,7 +427,7 @@
     out.wait()
 
 
-def attend(lengths, q, k, v, tokens, w_own, w_other):
+def attend(lengths, q, k, v, w_other, tokens, w_own):
     any_ = pl.BlockSpec(memory_space=pltpu.HBM)
     vm = pl.BlockSpec(memory_space=pltpu.VMEM)
     return pl.pallas_call(
@@ -450,26 +435,22 @@
         name="attend",
         out_shape=(
             jax.ShapeDtypeStruct((N, D), BF16),
-            jax.ShapeDtypeStruct((IMAGES, D), BF16),
+            pltpu.VMEM((IMAGES, D), BF16),
         ),
-        in_specs=[vm] + [any_] * 6,
+        in_specs=[vm] * 5 + [any_] * 2,
         out_specs=(any_, vm),
         scratch_shapes=[
             pltpu.VMEM((N, D), BF16),
-            pltpu.VMEM((3 * N, D), BF16),
-            pltpu.VMEM((3 * N, D), BF16),
-            pltpu.VMEM((N, D), BF16),
-            pltpu.VMEM((HALF, D), BF16),
             pltpu.VMEM((HALF, D), BF16),
             pltpu.VMEM((N, D), BF16),
             pltpu.VMEM((128, 128 * CLASSES[-1]), F32),
             pltpu.VMEM((N, D), BF16),
             pltpu.VMEM((N, 1), F32),
             pltpu.VMEM((1, 3 * N), F32),
-            pltpu.SemaphoreType.DMA((7,)),
+            pltpu.SemaphoreType.DMA((3,)),
         ],
-        compiler_params=pltpu.CompilerParams(vmem_limit_bytes=VMEM_LIMIT),
-    )(lengths, q, k, v, tokens, w_own, w_other)
+        compiler_params=pltpu.CompilerParams(vmem_limit_bytes=28 * MIB),
+    )(lengths, *[held(x) for x in (q, k, v, w_other)], outside(tokens), outside(w_own))
 
 
 def combine_kernel(
@@ -565,7 +546,7 @@
     return pl.pallas_call(
         combine_kernel,
         name="combine",
-        out_shape=jax.ShapeDtypeStruct((IMAGES, D), F32),
+        out_shape=pltpu.VMEM((IMAGES, D), F32),
         in_specs=[vm],
         out_specs=vm,
         scratch_shapes=[
@@ -588,14 +569,16 @@
             dma((3,)),
             dma((3,)),
         ],
-        compiler_params=pltpu.CompilerParams(collective_id=1, has_side_effects=True),
-    )(part)
+        compiler_params=pltpu.CompilerParams(
+            collective_id=1, has_side_effects=True, vmem_limit_bytes=8 * MIB
+        ),
+    )(held(part))
 
 
 def shards(tokens, lengths, ln_gain, w_qkv, w_out):
     rows = tokens.reshape(N, D)
     q, k, v, w_other = gather(rows, ln_gain, w_qkv, w_out)
-    hidden, part = attend(lengths, q, k, v, rows, w_out, w_other)
+    hidden, part = attend(lengths, q, k, v, w_other, rows, w_out)
     pooled = combine(part)
     return hidden.reshape(1, N, D), pooled.reshape(1, IMAGES, D)
 

time: 126 us -> 116 us (0.921)
  Pallas kernels: 122 us -> 113 us
    pallas_call x1, Pallas kernels: 21.7 us -> 16.2 us  [attend(): pl.pallas_call(attend_kernel, name='attend', out_shape=(jax.ShapeDtypeStr...]
    pallas_call x2, Pallas kernels: 100 us -> 96.9 us  [the longest x1 64.5 us: gather(): pl.pallas_call(gather_kernel, name='gather', out_shape=(pltpu.VMEM((N, D)...]
where the time goes in v3:
time: 116 us
  Pallas kernels  113 us (97%)
  local copies, waits for them, and re-layouts  1.75 us (2%)
    pallas_call x1, Pallas kernels, gather(): pl.pallas_call(gather_kernel, name='gather', out_shape=(pltpu.VMEM((N, D)...  64.5 us
    pallas_call x1, Pallas kernels, combine(): pl.pallas_call(combine_kernel, name='combine', out_shape=pltpu.VMEM((IMAG...  32.4 us
    pallas_call x1, Pallas kernels, attend(): pl.pallas_call(attend_kernel, name='attend', out_shape=(jax.ShapeDtypeStr...  16.2 us

profile of v3, /device:TPU:1, one launch (start us, length us, event | category | flops | bytes accessed | tf_op | source)
XLA Modules:
  0.0 115.5 jit_solution(15959438324558105605)
XLA Ops:
  0.6 0.0 copy-start
  0.6 0.7 copy-done
  1.3 0.0 copy-start.1
  1.3 64.5 %gather.1 = (bf16[512,1280]{1,0:T(8,128)(2,1)S(1)}, bf16[1536,1280]{1,0:T(8,128)(2,1)S(1)}, bf16[1536,1280]{1,0:T(8,128)(2,1)S(1)}, bf16[640,1280]{1,0:T(8,128)(2,1)S(1)}) custom-call(bf16[512,1280]{1,0:T(8,128)(2,1)} %bitcast.4, f32[1280]{0:T(1024)S(1)} %copy-done, bf16[640,3840]{1,0:T(8,128)(2,1)} %wq_hbm.1, bf16[640,1280]{1,0:T(8,128)(2,1)} %wa_hbm.1), custom_call_target="tpu_custom_call" | custom-call | tf_op jit(solution)/shard_map/gather/pallas_call | solution.py:284
  65.9 0.0 copy-done.1
  65.9 16.2 %attend.1 = (bf16[512,1280]{1,0:T(8,128)(2,1)}, bf16[256,1280]{1,0:T(8,128)(2,1)S(1)}) custom-call(s32[1,256]{1,0:T(1,128)S(1)} %copy-done.1, bf16[512,1280]{1,0:T(8,128)(2,1)S(1)} %get-tuple-element.8.q, bf16[1536,1280]{1,0:T(8,128)(2,1)S(1)} %get-tuple-element.9.k, bf16[1536,1280]{1,0:T(8,128)(2,1)S(1)} %get-tuple-element.10.v, ...), custom_call_target="tpu_custom_call" | custom-call | tf_op jit(solution)/shard_map/attend/pallas_call | solution.py:433
  82.1 32.4 %combine.1 = f32[256,1280]{1,0:T(8,128)S(1)} custom-call(bf16[256,1280]{1,0:T(8,128)(2,1)S(1)} %get-tuple-element.13.part), custom_call_target="tpu_custom_call" | custom-call | tf_op jit(solution)/shard_map/combine/pallas_call | solution.py:546
  114.5 1.1 copy.8
Async XLA Ops:
  0.6 0.7 copy-start
  1.3 64.6 %copy-start.1 = (s32[1,256]{1,0:T(1,128)S(1)}, s32[1,256]{1,0:T(1,128)}, u32[]{:S(2)}) copy-start(s32[1,256]{1,0:T(1,128)} %lens_ref.1) | copy-start | bytes 3076

commit v4 on v3

--- a/solution.py
+++ b/solution.py
@@ -18,7 +18,6 @@
 TOTAL = 32768
 SCALE = SIZE**-0.5 * math.log2(math.e)
 PIECE = 80
-UPPER = (0, 1, 2, 6)
 CLASSES = (2, 3, 4, 5, 6, 9)
 MIB = 1024 * 1024
 
@@ -39,7 +38,12 @@
         "core": (mate, sy, d),
         "z": (onward // 8, lax.rem(onward, 8), d),
         "zb": (back // 8, lax.rem(back, 8), d),
+        "zi": (sx, lax.rem(sy + 6 + 4 * h, 8), d),
+        "zj": (sx, lax.rem(sy + 10 - 4 * h, 8), d),
     }
+    z = sy // 2
+    first, last = (3 - z) // 3, z // 3
+    where["hop"] = (6 - 4 * h * first, 2 + 4 * (1 - h) * last)
     return sx, sy, d, h, mate, where
 
 
@@ -51,60 +55,74 @@
 
 
 class Exchange:
-    def __init__(self, refs, sx, where, send, recv):
-        self.refs, self.sx, self.where = refs, sx, where
-        self.send, self.recv = send, recv
-
-    def copy(self, kind, c):
-        own, other = self.refs[c // 6]
-        cols = pl.ds((c % 6) * HALF, HALF)
-        upper = c in UPPER
+    def __init__(self, own, other, sx, z, turn, where, send, recv):
+        self.own, self.other, self.sx, self.z, self.turn = own, other, sx, z, turn
+        self.where, self.send, self.recv = where, send, recv
+
+    def copy(self, kind, t, side):
+        pair = lax.rem(self.z + self.turn * (t - (kind == 8)) + 8, 4)
+        chunk = pair + 3 + pair // 3 if side else pair + 3 * (pair // 3)
+        cols = pl.ds(pl.multiple_of(chunk * HALF, 128), HALF)
+        own, other, where = self.own, self.other, self.where
+        hop = where["hop"][side] if t else (6, 2)[side]
         ahead, src, to = (
-            (0, own, "a" if upper else "b"),
-            (0, other, "xp"),
-            (0, other, "xm"),
-            (0, other, "core"),
-            (2, other, "xm") if upper else (6, other, "xp"),
-            (2, other, "core"),
-            (6, other, "core"),
-            (4, other, "core"),
+            (0, own, where["b" if side else "a"]),
+            (0, other, where["xp"]),
+            (0, other, where["xm"]),
+            (0, other, where["core"]),
+            (8 - hop, other, (lax.rem(self.sx + hop, 8),) + where["core"][1:]),
+            (2, other, where["core"]),
+            (6, other, where["core"]),
+            (4, other, where["core"]),
+            (0, other, where["zi"]),
         )[kind]
         rows = pl.ds(pl.multiple_of(lax.rem(self.sx + ahead, 8) * PIECE, 16), PIECE)
+        i = kind * 8 + side * 4 + t
         return pltpu.make_async_remote_copy(
             src_ref=src.at[rows, cols],
             dst_ref=other.at[rows, cols],
-            send_sem=self.send.at[kind * 8 + c],
-            recv_sem=self.recv.at[kind * 8 + c],
-            device_id=self.where[to],
+            send_sem=self.send.at[i],
+            recv_sem=self.recv.at[i],
+            device_id=to,
             device_id_type=MESH,
         )
 
-    def step(self, cs, waits, goes):
-        for c in cs:
-            for kind in waits:
-                self.copy(kind, c).wait_recv()
-            for kind in goes:
-                self.copy(kind, c).start()
-
-    def begin(self, *cs):
-        self.step(cs, (), (0,))
-
-    def from_y(self, *cs):
-        self.step(cs, (0,), (1, 2, 3))
-
-    def from_x(self, *cs):
-        self.step(cs, (1, 2), (4, 5, 6))
-
-    def from_far(self, *cs):
-        self.step(cs, (4,), (7,))
-
-    def finish(self, *cs):
-        self.step(cs, (3, 5, 6, 7), ())
+    def begin(self):
+        for side in range(2):
+            self.copy(0, 0, side).start()
+
+    def landed(self, t):
+        for side in range(2):
+            self.copy(8 if t else 0, t, side).wait_recv()
+            if t < 3:
+                self.copy(8, t + 1, side).start()
+            for kind in (1, 2, 3):
+                self.copy(kind, t, side).start()
+
+    def from_x(self, t):
+        for side in range(2):
+            for kind in (1, 2):
+                self.copy(kind, t, side).wait_recv()
+            for kind in (4, 5, 6):
+                self.copy(kind, t, side).start()
+
+    def from_far(self, t):
+        for side in range(2):
+            self.copy(4, t, side).wait_recv()
+            self.copy(7, t, side).start()
+
+    def finish(self):
+        for t in range(4):
+            for side in range(2):
+                for kind in (3, 5, 6, 7):
+                    self.copy(kind, t, side).wait_recv()
 
     def sent(self):
-        for c in range(8):
-            for kind in range(8):
-                self.copy(kind, c).wait_send()
+        for side in range(2):
+            for t in range(4):
+                for kind in range(1, 8):
+                    self.copy(kind, t, side).wait_send()
+                self.copy(8 if t else 0, t, side).wait_send()
 
 
 class Halo:
@@ -154,22 +172,26 @@
 
 def gather_kernel(
     tok_hbm, gain_ref, wq_hbm, wo_hbm,
-    qs, ks, vs, woo,
-    tok, wq, wqo, near, far, ta, tb, nrm, nrm2, acc,
+    qs, ks, vs, wall,
+    tok, wown, near, far, ta, tb, nrm, nrmh, acc, acch,
     w_send, w_recv, h_send, h_recv, local,
 ):
     sx, sy, d, h, mate, where = places()
+    wq_in = pltpu.make_async_copy(wq_hbm, wown.at[:, pl.ds(0, 3 * D)], local.at[1])
+    wo_in = pltpu.make_async_copy(wo_hbm, wown.at[:, pl.ds(3 * D, D)], local.at[2])
+    tok_in = pltpu.make_async_copy(tok_hbm, tok, local.at[0])
+    wq_in.start()
+    wo_in.start()
+    tok_in.start()
     barrier = pltpu.get_barrier_semaphore()
-    for name in ("a", "b", "xp", "xm", "core", "z", "zb"):
+    partners = ("a", "b", "xp", "xm", "core", "z", "zb", "zi", "zj")
+    for name in partners:
         pl.semaphore_signal(barrier, inc=1, device_id=where[name], device_id_type=MESH)
-
-    tok_in = pltpu.make_async_copy(tok_hbm, tok, local.at[0])
-    wq_in = pltpu.make_async_copy(wq_hbm, wq, local.at[1])
-    tok_in.start()
-    wq_in.start()
-    pl.semaphore_wait(barrier, 7)
-
-    weights = Exchange(((wq_hbm, wqo), (wo_hbm, woo)), sx, where, w_send, w_recv)
+    wq_in.wait()
+    wo_in.wait()
+    pl.semaphore_wait(barrier, len(partners))
+
+    weights = Exchange(wown, wall, sx, sy // 2, 1 - 2 * h, where, w_send, w_recv)
     halo = Halo(tok_hbm, ta, tb, near, far, where, h_send, h_recv)
     gain = gain_ref[...].reshape(1, D)
     mine = pl.ds(pl.multiple_of(d * HALF, 128), HALF)
@@ -186,7 +208,7 @@
         def one(i, _):
             rows = pl.ds(pl.multiple_of(i * 256, 256), 256)
             cols = pl.ds(part * D, D)
-            acc[rows, cols] = jnp.dot(nrm[rows, mine], wq[:, cols], preferred_element_type=F32)
+            acc[rows, cols] = jnp.dot(nrm[rows, mine], wown[:, cols], preferred_element_type=F32)
             return 0
 
         lax.fori_loop(0, 2, one, 0)
@@ -196,75 +218,92 @@
         into = pl.ds(pl.multiple_of(N + i * 256, 256), 256)
         for part, ref, at, factor in ((0, qs, rows, SCALE), (1, ks, into, None), (2, vs, into, None)):
             cols = pl.ds(part * D, D)
-            value = acc[rows, cols] + jnp.dot(nrm[rows, others], wqo[:, cols], preferred_element_type=F32)
+            value = acc[rows, cols] + jnp.dot(nrm[rows, others], wall[:, cols], preferred_element_type=F32)
             if factor is not None:
                 value = value * factor
             ref[at, :] = value.astype(BF16)
         return 0
 
-    def keyvals(src, first, base):
-        for j in range(4):
-            rows = src[pl.ds(128 * (first + 2 * (j // 2)) + 64 * (j % 2), 64), :]
-            nrm2[pl.ds(64 * j, 64), :] = normalize(rows, gain)
-        for part, ref in ((1, ks), (2, vs)):
-            cols = pl.ds(part * D, D)
-            value = jnp.dot(nrm2[:, mine], wq[:, cols], preferred_element_type=F32)
-            value = value + jnp.dot(nrm2[:, others], wqo[:, cols], preferred_element_type=F32)
+    def halo_first(src, first, group):
+        def one(j, _):
+            at = pl.multiple_of(128 * first + 64 * lax.rem(j, 2) + 256 * (j // 2), 64)
+            to = pl.multiple_of(256 * group + 64 * j, 64)
+            nrmh[pl.ds(to, 64), :] = normalize(src[pl.ds(at, 64), :], gain)
+            return 0
+
+        lax.fori_loop(0, 4, one, 0)
+        rows = pl.ds(256 * group, 256)
+        for part in range(2):
+            acch[rows, pl.ds(part * D, D)] = jnp.dot(
+                nrmh[rows, mine], wown[:, pl.ds((part + 1) * D, D)], preferred_element_type=F32
+            )
+
+    def halo_second(first, base, group):
+        rows = pl.ds(256 * group, 256)
+        for part, ref in ((0, ks), (1, vs)):
+            value = acch[rows, pl.ds(part * D, D)] + jnp.dot(
+                nrmh[rows, others], wall[:, pl.ds((part + 1) * D, D)], preferred_element_type=F32
+            )
             for j in range(2):
-                start = pl.multiple_of(base + 128 * (first + 2 * j), 128)
+                start = pl.multiple_of(base + 128 * first + 256 * j, 128)
                 ref[pl.ds(start, 128), :] = value[128 * j : 128 * j + 128].astype(BF16)
 
-    with jax.named_scope("g0_start"):
-        weights.begin(0, 3, 1, 4, 2, 5)
+    with jax.named_scope("g0"):
+        weights.begin()
         halo.own(0)
         halo.own(1)
         tok_in.wait()
         lax.fori_loop(0, N // 64, norm_own, 0)
-        weights.from_y(0, 3)
-        wq_in.wait()
+        weights.landed(0)
         first_half(0)
-        weights.from_y(1, 4)
-        first_half(1)
-        weights.from_y(2, 5)
-        first_half(2)
-    with jax.named_scope("g1_relay0"):
+    with jax.named_scope("g1"):
         halo.relay(0)
         halo.own(2)
-        weights.from_x(0, 3, 1)
-    with jax.named_scope("g2_relay1"):
+        first_half(1)
+        weights.landed(1)
+    with jax.named_scope("g2"):
         halo.relay(1)
-        weights.begin(6, 7)
         halo.own(3)
-        weights.from_x(4, 2, 5)
+        first_half(2)
+        weights.landed(2)
+    with jax.named_scope("g3"):
         halo.onward(0)
-    with jax.named_scope("g3_relay2"):
+        weights.from_x(0)
+        weights.landed(3)
+    with jax.named_scope("g4"):
         halo.relay(2)
+        weights.from_x(1)
         halo.onward(1)
-        weights.from_far(0, 3, 1, 4, 2, 5)
+        weights.from_x(2)
+    with jax.named_scope("g5"):
+        halo_first(near, 0, 0)
         halo.relay(3)
-    with jax.named_scope("g4_weights"):
-        weights.finish(0, 3, 1, 4, 2, 5)
-        weights.from_y(6, 7)
-    with jax.named_scope("g5_own"):
-        lax.fori_loop(0, 2, second_half, 0)
-    with jax.named_scope("g6_near2"):
+    with jax.named_scope("g6"):
+        weights.from_far(0)
+        weights.from_x(3)
         halo.onward(2)
-        weights.from_x(6, 7)
-        keyvals(near, 0, near_at)
-    with jax.named_scope("g7_near3"):
+        weights.from_far(1)
         halo.onward(3)
-        weights.from_far(6, 7)
-        keyvals(near, 1, near_at)
-    with jax.named_scope("g8_far1"):
+    with jax.named_scope("g7"):
+        weights.from_far(2)
+        halo_first(near, 1, 1)
+    with jax.named_scope("g8"):
+        weights.from_far(3)
         halo.arrived(0)
         halo.arrived(1)
-        keyvals(far, 0, far_at)
-        weights.finish(6, 7)
-    with jax.named_scope("g9_far3"):
+        halo_first(far, 0, 2)
+        weights.finish()
+    with jax.named_scope("g9"):
+        lax.fori_loop(0, 2, second_half, 0)
+        halo_second(0, near_at, 0)
+        halo_second(1, near_at, 1)
+        halo_second(0, far_at, 2)
+    with jax.named_scope("g12"):
         halo.arrived(2)
         halo.arrived(3)
-    with jax.named_scope("g10_end"):
-        keyvals(far, 1, far_at)
+    with jax.named_scope("g13"):
+        halo_first(far, 1, 0)
+        halo_second(1, far_at, 0)
         weights.sent()
         halo.sent()
 
@@ -288,29 +327,29 @@
             pltpu.VMEM((N, D), BF16),
             pltpu.VMEM((3 * N, D), BF16),
             pltpu.VMEM((3 * N, D), BF16),
-            pltpu.VMEM((HALF, D), BF16),
+            pltpu.VMEM((HALF, 4 * D), BF16),
         ),
         in_specs=[any_, vm, any_, any_],
         out_specs=(vm,) * 4,
         scratch_shapes=[
             pltpu.VMEM((N, D), BF16),
-            pltpu.VMEM((HALF, 3 * D), BF16),
-            pltpu.VMEM((HALF, 3 * D), BF16),
+            pltpu.VMEM((HALF, 4 * D), BF16),
             pltpu.VMEM((N, D), BF16),
             pltpu.VMEM((N, D), BF16),
             pltpu.VMEM((256, D), BF16),
             pltpu.VMEM((256, D), BF16),
             pltpu.VMEM((N, D), BF16),
-            pltpu.VMEM((256, D), BF16),
+            pltpu.VMEM((768, D), BF16),
             pltpu.VMEM((N, 3 * D), F32),
-            dma((64,)),
-            dma((64,)),
+            pltpu.VMEM((768, 2 * D), F32),
+            dma((72,)),
+            dma((72,)),
             dma((24,)),
             dma((24,)),
-            dma((2,)),
+            dma((3,)),
         ],
         compiler_params=pltpu.CompilerParams(
-            collective_id=0, has_side_effects=True, vmem_limit_bytes=40 * MIB
+            collective_id=0, has_side_effects=True, vmem_limit_bytes=44 * MIB
         ),
     )(outside(tokens), gain, outside(w_qkv), outside(w_out))
 
@@ -368,9 +407,12 @@
                 keys = pl.ds(start, n)
                 bias[:, pl.ds(0, n)] = jnp.where(ids == kid[:, keys], 0.0, -1e30)
 
-                def two_pairs(pp, _):
-                    for sub in range(2):
-                        pair = pp * 2 + sub
+                several = 4 if size < 6 else 2
+
+                def pairs(group, _):
+                    work = []
+                    for sub in range(several):
+                        pair = group * several + sub
                         tile = (pair * 5) >> 2
                         lanes = pl.ds(pl.multiple_of(tile * 128, 128), 256)
                         shift = pair * 160 - tile * 128
@@ -388,18 +430,22 @@
                         scores = lax.dot_general(
                             both, k[keys, lanes], (((1,), (1,)), ((), ())), preferred_element_type=F32
                         )
+                        work.append((lanes, one, two, scores))
+                    done = []
+                    for lanes, one, two, scores in work:
                         extra = bias[:, pl.ds(0, n)]
                         scores = scores + jnp.concatenate([extra, extra], axis=0)
                         top = jnp.max(scores, axis=1, keepdims=True)
                         weights = jnp.exp2(scores - top)
                         total = jnp.sum(weights, axis=1, keepdims=True)
                         mixed = jnp.dot(weights.astype(BF16), v[keys, lanes], preferred_element_type=F32)
-                        mixed = mixed * (1.0 / total)
+                        done.append((lanes, one, two, mixed * (1.0 / total)))
+                    for lanes, one, two, mixed in done:
                         old = ctx[rows, lanes].astype(F32)
                         ctx[rows, lanes] = jnp.where(one, mixed[:128], jnp.where(two, mixed[128:], old)).astype(BF16)
                     return 0
 
-                lax.fori_loop(0, 4, two_pairs, 0)
+                lax.fori_loop(0, 8 // several, pairs, 0)
 
             before = size
         return 0
@@ -413,7 +459,7 @@
     def project(i, _):
         rows = pl.ds(pl.multiple_of(i * 256, 256), 256)
         mixed = jnp.dot(ctx[rows, mine], wa[...], preferred_element_type=F32)
-        mixed = mixed + jnp.dot(ctx[rows, others], wb[...], preferred_element_type=F32)
+        mixed = mixed + jnp.dot(ctx[rows, others], wb[:, pl.ds(3 * D, D)], preferred_element_type=F32)
         hid[rows, :] = (tok[rows, :].astype(F32) + mixed).astype(BF16)
         return 0
 

time: 116 us -> 111 us (0.957); the launches traced: 116 us -> 112 us
  Pallas kernels: 113 us -> 110 us
    pallas_call x1, Pallas kernels: 16.2 us -> 12.6 us  [attend(): pl.pallas_call(attend_kernel, name='attend', out_shape=(jax.ShapeDtypeStr...]
    pallas_call x1, Pallas kernels: 32.4 us -> 34 us  [combine(): pl.pallas_call(combine_kernel, name='combine', out_shape=pltpu.VMEM((IMAG...]
    pallas_call x1, Pallas kernels: 64.5 us -> 63.4 us  [gather(): pl.pallas_call(gather_kernel, name='gather', out_shape=(pltpu.VMEM((N, D)...]
where the time goes in v4:
time: 111 us; the launch traced here: 112 us
  Pallas kernels  110 us (99%)
    pallas_call x1, Pallas kernels, gather(): pl.pallas_call(gather_kernel, name='gather', out_shape=(pltpu.VMEM((N, D)...  63.4 us
    pallas_call x1, Pallas kernels, combine(): pl.pallas_call(combine_kernel, name='combine', out_shape=pltpu.VMEM((IMAG...  34 us
    pallas_call x1, Pallas kernels, attend(): pl.pallas_call(attend_kernel, name='attend', out_shape=(jax.ShapeDtypeStr...  12.6 us

profile of v4, /device:TPU:1, one launch (start us, length us, event | category | flops | bytes accessed | tf_op | source)
XLA Modules:
  0.0 111.7 jit_solution(11582642529674450618)
XLA Ops:
  0.6 0.0 copy-start
  0.6 63.4 %gather.1 = (bf16[512,1280]{1,0:T(8,128)(2,1)S(1)}, bf16[1536,1280]{1,0:T(8,128)(2,1)S(1)}, bf16[1536,1280]{1,0:T(8,128)(2,1)S(1)}, bf16[640,5120]{1,0:T(8,128)(2,1)S(1)}) custom-call(bf16[512,1280]{1,0:T(8,128)(2,1)} %bitcast.4, f32[1280]{0:T(1024)} %gain_ref.1, bf16[640,3840]{1,0:T(8,128)(2,1)} %wq_hbm.1, bf16[640,1280]{1,0:T(8,128)(2,1)} %wa_hbm.1), custom_call_target="tpu_custom_call" | custom-call | tf_op jit(solution)/shard_map/gather/pallas_call | solution.py:323
  64.0 0.0 copy-done
  64.0 12.6 %attend.1 = (bf16[512,1280]{1,0:T(8,128)(2,1)}, bf16[256,1280]{1,0:T(8,128)(2,1)S(1)}) custom-call(s32[1,256]{1,0:T(1,128)S(1)} %copy-done, bf16[512,1280]{1,0:T(8,128)(2,1)S(1)} %get-tuple-element.8.q, bf16[1536,1280]{1,0:T(8,128)(2,1)S(1)} %get-tuple-element.9.k, bf16[1536,1280]{1,0:T(8,128)(2,1)S(1)} %get-tuple-element.10.v, ...), custom_call_target="tpu_custom_call" | custom-call | tf_op jit(solution)/shard_map/attend/pallas_call | solution.py:479
  76.6 34.0 %combine.1 = f32[256,1280]{1,0:T(8,128)S(1)} custom-call(bf16[256,1280]{1,0:T(8,128)(2,1)S(1)} %get-tuple-element.13.part), custom_call_target="tpu_custom_call" | custom-call | tf_op jit(solution)/shard_map/combine/pallas_call | solution.py:592
  110.7 1.1 copy.8
Async XLA Ops:
  0.6 63.4 %copy-start = (s32[1,256]{1,0:T(1,128)S(1)}, s32[1,256]{1,0:T(1,128)}, u32[]{:S(2)}) copy-start(s32[1,256]{1,0:T(1,128)} %lens_ref.1) | copy-start | bytes 3076

commit v5 on v4

--- a/solution.py
+++ b/solution.py
@@ -430,12 +430,11 @@
                         scores = lax.dot_general(
                             both, k[keys, lanes], (((1,), (1,)), ((), ())), preferred_element_type=F32
                         )
-                        work.append((lanes, one, two, scores))
-                    done = []
-                    for lanes, one, two, scores in work:
                         extra = bias[:, pl.ds(0, n)]
                         scores = scores + jnp.concatenate([extra, extra], axis=0)
-                        top = jnp.max(scores, axis=1, keepdims=True)
+                        work.append((lanes, one, two, scores, jnp.max(scores, axis=1, keepdims=True)))
+                    done = []
+                    for lanes, one, two, scores, top in work:
                         weights = jnp.exp2(scores - top)
                         total = jnp.sum(weights, axis=1, keepdims=True)
                         mixed = jnp.dot(weights.astype(BF16), v[keys, lanes], preferred_element_type=F32)
@@ -499,10 +498,7 @@
     )(lengths, *[held(x) for x in (q, k, v, w_other)], outside(tokens), outside(w_own))
 
 
-def combine_kernel(
-    part, out, rc, one, rx, two, ry, three, four, last,
-    c_send, c_recv, x_send, x_recv, y_send, y_recv, g_send, g_recv, w_send, w_recv,
-):
+def combine_kernel(part, out, rc, one, rx, two, ry, three, strip32, four, last, send, recv):
     sx, sy, d = lax.axis_index("sx"), lax.axis_index("sy"), lax.axis_index("dp")
     core = lax.rem(sx, 2)
     chip = sx // 2
@@ -514,76 +510,90 @@
         pl.semaphore_signal(barrier, inc=1, device_id=who, device_id_type=MESH)
     pl.semaphore_wait(barrier, 11)
 
-    def remote(src, dst, send, recv, who):
-        return pltpu.make_async_remote_copy(
-            src_ref=src, dst_ref=dst, send_sem=send, recv_sem=recv, device_id=who, device_id_type=MESH
-        )
-
     my_half = pl.ds(pl.multiple_of(core * 128, 128), 128)
     its_half = pl.ds(pl.multiple_of((1 - core) * 128, 128), 128)
-    c_copy = remote(part.at[its_half], rc, c_send.at[0], c_recv.at[0], mate)
-    c_copy.start()
-    c_copy.wait_recv()
-    one[...] = (part[my_half, :].astype(F32) + rc[...].astype(F32)).astype(BF16)
-
-    def strip(owner):
-        return pl.ds(pl.multiple_of(owner * 32, 32), 32)
-
-    x_copies = [
-        remote(one.at[strip(lax.rem(chip + j, 4))], rx.at[j - 1], x_send.at[j - 1], x_recv.at[j - 1], chips[j - 1])
-        for j in (1, 2, 3)
-    ]
-    for copy in x_copies:
-        copy.start()
-    for copy in x_copies:
-        copy.wait_recv()
-    total = one[strip(chip), :].astype(F32)
-    for j in range(3):
-        total = total + rx[j].astype(F32)
-    for j in range(2):
-        two[j] = total[:, j * HALF : (j + 1) * HALF]
-
-    def spot(owner):
-        return pl.ds(pl.multiple_of((owner // 2) * 8, 8), 8)
-
-    y_copies = []
-    for j in range(1, 8):
-        to = lax.rem(sy + j, 8)
-        y_copies.append(
-            remote(two.at[lax.rem(to, 2), spot(to)], ry.at[j - 1], y_send.at[j - 1], y_recv.at[j - 1], plane[j - 1])
+    halves = [pl.ds(half * HALF, HALF) for half in range(2)]
+
+    def strip(ahead):
+        return pl.ds(pl.multiple_of(lax.rem(chip + ahead, 4) * 32, 32), 32)
+
+    def remote(i, half, src, dst, who):
+        return pltpu.make_async_remote_copy(
+            src_ref=src,
+            dst_ref=dst,
+            send_sem=send.at[25 * half + i],
+            recv_sem=recv.at[25 * half + i],
+            device_id=who,
+            device_id_type=MESH,
         )
-    for copy in y_copies:
-        copy.start()
-    for copy in y_copies:
-        copy.wait_recv()
-    side = lax.rem(sy, 2)
-    total = two[side, spot(sy), :]
-    for j in range(7):
-        total = total + ry[j]
-    three[side, spot(sy), :] = total
-    g_copies = [
-        remote(three.at[side, spot(sy)], three.at[side, spot(sy)], g_send.at[j], g_recv.at[j], plane[j])
-        for j in range(7)
-    ]
-    for copy in g_copies:
-        copy.start()
-    for copy in g_copies:
-        copy.wait_recv()
-    four[strip(chip), :] = jnp.concatenate([three[0], three[1]], axis=1).astype(BF16)
-    w_copies = [
-        remote(four.at[strip(chip)], four.at[strip(chip)], w_send.at[j], w_recv.at[j], chips[j]) for j in range(3)
-    ]
-    for copy in w_copies:
-        copy.start()
-    for copy in w_copies:
-        copy.wait_recv()
-    l_copy = remote(four, last, c_send.at[1], c_recv.at[1], mate)
-    l_copy.start()
-    out[my_half, :] = four[...].astype(F32)
-    l_copy.wait_recv()
-    out[its_half, :] = last[...].astype(F32)
-    for copy in [c_copy, l_copy] + x_copies + y_copies + g_copies + w_copies:
-        copy.wait_send()
+
+    copies = {}
+    for half in range(2):
+        copies["c", half] = [remote(0, half, part.at[its_half, halves[half]], rc.at[half], mate)]
+        copies["x", half] = [
+            remote(j, half, one.at[half, strip(j)], rx.at[half, j - 1], chips[j - 1]) for j in (1, 2, 3)
+        ]
+        copies["p", half] = [
+            remote(3 + j, half, two.at[half, lax.rem(sy + j, 8)], ry.at[half, j - 1], plane[j - 1])
+            for j in range(1, 8)
+        ]
+        copies["g", half] = [
+            remote(10 + j, half, three.at[half, sy], three.at[half, sy], plane[j - 1]) for j in range(1, 8)
+        ]
+        copies["w", half] = [
+            remote(17 + j, half, four.at[half, strip(0)], four.at[half, strip(0)], chips[j - 1]) for j in (1, 2, 3)
+        ]
+        copies["m", half] = [
+            remote(21 + j, half, four.at[half, strip(4 - j)], last.at[half, strip(4 - j)], mate) for j in range(4)
+        ]
+
+    def go(name, half):
+        for copy in copies[name, half]:
+            copy.start()
+
+    def arrived(name, half):
+        for copy in copies[name, half]:
+            copy.wait_recv()
+
+    for half in range(2):
+        go("c", half)
+    for half in range(2):
+        arrived("c", half)
+        one[half] = (part[my_half, halves[half]].astype(F32) + rc[half].astype(F32)).astype(BF16)
+        go("x", half)
+    for half in range(2):
+        arrived("x", half)
+        total = one[half, strip(0), :].astype(F32)
+        for j in range(3):
+            total = total + rx[half, j].astype(F32)
+        for j in range(8):
+            two[half, j] = total[4 * j : 4 * j + 4]
+        go("p", half)
+    for half in range(2):
+        arrived("p", half)
+        total = two[half, sy]
+        for j in range(7):
+            total = total + ry[half, j]
+        three[half, sy] = total
+        go("g", half)
+    for half in range(2):
+        arrived("g", half)
+        for j in range(8):
+            strip32[pl.ds(4 * j, 4), :] = three[half, j]
+        four[half, strip(0), :] = strip32[...].astype(BF16)
+        go("w", half)
+        copies["m", half][0].start()
+    for half in range(2):
+        for j in (1, 3, 2):
+            copies["w", half][j - 1].wait_recv()
+            copies["m", half][j].start()
+        out[my_half, halves[half]] = four[half].astype(F32)
+    for half in range(2):
+        arrived("m", half)
+        out[its_half, halves[half]] = last[half].astype(F32)
+    for group in copies.values():
+        for copy in group:
+            copy.wait_send()
 
 
 def combine(part):
@@ -596,24 +606,17 @@
         in_specs=[vm],
         out_specs=vm,
         scratch_shapes=[
-            pltpu.VMEM((128, D), BF16),
-            pltpu.VMEM((128, D), BF16),
-            pltpu.VMEM((3, 32, D), BF16),
-            pltpu.VMEM((2, 32, HALF), F32),
-            pltpu.VMEM((7, 8, HALF), F32),
-            pltpu.VMEM((2, 32, HALF), F32),
-            pltpu.VMEM((128, D), BF16),
-            pltpu.VMEM((128, D), BF16),
-            dma((2,)),
-            dma((2,)),
-            dma((3,)),
-            dma((3,)),
-            dma((7,)),
-            dma((7,)),
-            dma((7,)),
-            dma((7,)),
-            dma((3,)),
-            dma((3,)),
+            pltpu.VMEM((2, 128, HALF), BF16),
+            pltpu.VMEM((2, 128, HALF), BF16),
+            pltpu.VMEM((2, 3, 32, HALF), BF16),
+            pltpu.VMEM((2, 8, 4, HALF), F32),
+            pltpu.VMEM((2, 7, 4, HALF), F32),
+            pltpu.VMEM((2, 8, 4, HALF), F32),
+            pltpu.VMEM((32, HALF), F32),
+            pltpu.VMEM((2, 128, HALF), BF16),
+            pltpu.VMEM((2, 128, HALF), BF16),
+            dma((50,)),
+            dma((50,)),
         ],
         compiler_params=pltpu.CompilerParams(
             collective_id=1, has_side_effects=True, vmem_limit_bytes=8 * MIB

time: 111 us -> 108 us (0.973)
  Pallas kernels: 110 us -> 106 us
    pallas_call x1, Pallas kernels: 34 us -> 25.1 us  [combine(): pl.pallas_call(combine_kernel, name='combine', out_shape=pltpu.VMEM((IMAG...]
    pallas_call x1, Pallas kernels: 12.6 us -> 17.5 us  [attend(): pl.pallas_call(attend_kernel, name='attend', out_shape=(jax.ShapeDtypeStr...]
where the time goes in v5:
time: 108 us
  Pallas kernels  106 us (98%)
    pallas_call x1, Pallas kernels, gather(): pl.pallas_call(gather_kernel, name='gather', out_shape=(pltpu.VMEM((N, D)...  63.4 us
    pallas_call x1, Pallas kernels, combine(): pl.pallas_call(combine_kernel, name='combine', out_shape=pltpu.VMEM((IMAG...  25.1 us
    pallas_call x1, Pallas kernels, attend(): pl.pallas_call(attend_kernel, name='attend', out_shape=(jax.ShapeDtypeStr...  17.5 us

profile of v5, /device:TPU:1, one launch (start us, length us, event | category | flops | bytes accessed | tf_op | source)
XLA Modules:
  0.0 107.7 jit_solution(12511837324481715140)
XLA Ops:
  0.6 0.0 copy-start
  0.6 63.4 %gather.1 = (bf16[512,1280]{1,0:T(8,128)(2,1)S(1)}, bf16[1536,1280]{1,0:T(8,128)(2,1)S(1)}, bf16[1536,1280]{1,0:T(8,128)(2,1)S(1)}, bf16[640,5120]{1,0:T(8,128)(2,1)S(1)}) custom-call(bf16[512,1280]{1,0:T(8,128)(2,1)} %bitcast.4, f32[1280]{0:T(1024)} %gain_ref.1, bf16[640,3840]{1,0:T(8,128)(2,1)} %wq_hbm.1, bf16[640,1280]{1,0:T(8,128)(2,1)} %wa_hbm.1), custom_call_target="tpu_custom_call" | custom-call | tf_op jit(solution)/shard_map/gather/pallas_call | solution.py:323
  64.0 0.0 copy-done
  64.0 17.5 %attend.1 = (bf16[512,1280]{1,0:T(8,128)(2,1)}, bf16[256,1280]{1,0:T(8,128)(2,1)S(1)}) custom-call(s32[1,256]{1,0:T(1,128)S(1)} %copy-done, bf16[512,1280]{1,0:T(8,128)(2,1)S(1)} %get-tuple-element.8.q, bf16[1536,1280]{1,0:T(8,128)(2,1)S(1)} %get-tuple-element.9.k, bf16[1536,1280]{1,0:T(8,128)(2,1)S(1)} %get-tuple-element.10.v, ...), custom_call_target="tpu_custom_call" | custom-call | tf_op jit(solution)/shard_map/attend/pallas_call | solution.py:478
  81.5 25.1 %combine.1 = f32[256,1280]{1,0:T(8,128)S(1)} custom-call(bf16[256,1280]{1,0:T(8,128)(2,1)S(1)} %get-tuple-element.13.part), custom_call_target="tpu_custom_call" | custom-call | tf_op jit(solution)/shard_map/combine/pallas_call | solution.py:602
  106.6 1.1 copy.8
Async XLA Ops:
  0.6 63.4 %copy-start = (s32[1,256]{1,0:T(1,128)S(1)}, s32[1,256]{1,0:T(1,128)}, u32[]{:S(2)}) copy-start(s32[1,256]{1,0:T(1,128)} %lens_ref.1) | copy-start | bytes 3076

commit v6 on v5

--- a/solution.py
+++ b/solution.py
@@ -407,11 +407,12 @@
                 keys = pl.ds(start, n)
                 bias[:, pl.ds(0, n)] = jnp.where(ids == kid[:, keys], 0.0, -1e30)
 
-                several = 4 if size < 6 else 2
+                several = 8 if size < 6 else 4
 
                 def pairs(group, _):
-                    work = []
-                    for sub in range(several):
+                    work, soft = {}, {}
+
+                    def first(sub):
                         pair = group * several + sub
                         tile = (pair * 5) >> 2
                         lanes = pl.ds(pl.multiple_of(tile * 128, 128), 256)
@@ -432,16 +433,28 @@
                         )
                         extra = bias[:, pl.ds(0, n)]
                         scores = scores + jnp.concatenate([extra, extra], axis=0)
-                        work.append((lanes, one, two, scores, jnp.max(scores, axis=1, keepdims=True)))
-                    done = []
-                    for lanes, one, two, scores, top in work:
+                        work[sub] = (lanes, one, two, scores, jnp.max(scores, axis=1, keepdims=True))
+
+                    def middle(sub):
+                        lanes, one, two, scores, top = work.pop(sub)
                         weights = jnp.exp2(scores - top)
                         total = jnp.sum(weights, axis=1, keepdims=True)
-                        mixed = jnp.dot(weights.astype(BF16), v[keys, lanes], preferred_element_type=F32)
-                        done.append((lanes, one, two, mixed * (1.0 / total)))
-                    for lanes, one, two, mixed in done:
+                        soft[sub] = (lanes, one, two, weights.astype(BF16), total)
+
+                    def final(sub):
+                        lanes, one, two, weights, total = soft.pop(sub)
+                        mixed = jnp.dot(weights, v[keys, lanes], preferred_element_type=F32) * (1.0 / total)
                         old = ctx[rows, lanes].astype(F32)
                         ctx[rows, lanes] = jnp.where(one, mixed[:128], jnp.where(two, mixed[128:], old)).astype(BF16)
+
+                    first(0)
+                    for sub in range(several):
+                        if sub + 1 < several:
+                            first(sub + 1)
+                        middle(sub)
+                        if sub:
+                            final(sub - 1)
+                    final(several - 1)
                     return 0
 
                 lax.fori_loop(0, 8 // several, pairs, 0)

time: 108 us -> 105 us (0.972)
  Pallas kernels: 106 us -> 103 us
    pallas_call x1, Pallas kernels: 17.5 us -> 13.2 us  [attend(): pl.pallas_call(attend_kernel, name='attend', out_shape=(jax.ShapeDtypeStr...]
    pallas_call x1, Pallas kernels: 25.1 us -> 26.8 us  [combine(): pl.pallas_call(combine_kernel, name='combine', out_shape=pltpu.VMEM((IMAG...]
where the time goes in v6:
time: 105 us
  Pallas kernels  103 us (98%)
  local copies, waits for them, and re-layouts  1.06 us (1%)
    pallas_call x1, Pallas kernels, gather(): pl.pallas_call(gather_kernel, name='gather', out_shape=(pltpu.VMEM((N, D)...  63.4 us
    pallas_call x1, Pallas kernels, combine(): pl.pallas_call(combine_kernel, name='combine', out_shape=pltpu.VMEM((IMAG...  26.8 us
    pallas_call x1, Pallas kernels, attend(): pl.pallas_call(attend_kernel, name='attend', out_shape=(jax.ShapeDtypeStr...  13.2 us

profile of v6, /device:TPU:1, one launch (start us, length us, event | category | flops | bytes accessed | tf_op | source)
XLA Modules:
  0.0 105.1 jit_solution(2624109515979932380)
XLA Ops:
  0.6 0.0 copy-start
  0.6 63.4 %gather.1 = (bf16[512,1280]{1,0:T(8,128)(2,1)S(1)}, bf16[1536,1280]{1,0:T(8,128)(2,1)S(1)}, bf16[1536,1280]{1,0:T(8,128)(2,1)S(1)}, bf16[640,5120]{1,0:T(8,128)(2,1)S(1)}) custom-call(bf16[512,1280]{1,0:T(8,128)(2,1)} %bitcast.4, f32[1280]{0:T(1024)} %gain_ref.1, bf16[640,3840]{1,0:T(8,128)(2,1)} %wq_hbm.1, bf16[640,1280]{1,0:T(8,128)(2,1)} %wa_hbm.1), custom_call_target="tpu_custom_call" | custom-call | tf_op jit(solution)/shard_map/gather/pallas_call | solution.py:323
  64.0 0.0 copy-done
  64.0 13.2 %attend.1 = (bf16[512,1280]{1,0:T(8,128)(2,1)}, bf16[256,1280]{1,0:T(8,128)(2,1)S(1)}) custom-call(s32[1,256]{1,0:T(1,128)S(1)} %copy-done, bf16[512,1280]{1,0:T(8,128)(2,1)S(1)} %get-tuple-element.8.q, bf16[1536,1280]{1,0:T(8,128)(2,1)S(1)} %get-tuple-element.9.k, bf16[1536,1280]{1,0:T(8,128)(2,1)S(1)} %get-tuple-element.10.v, ...), custom_call_target="tpu_custom_call" | custom-call | tf_op jit(solution)/shard_map/attend/pallas_call | solution.py:491
  77.2 26.8 %combine.1 = f32[256,1280]{1,0:T(8,128)S(1)} custom-call(bf16[256,1280]{1,0:T(8,128)(2,1)S(1)} %get-tuple-element.13.part), custom_call_target="tpu_custom_call" | custom-call | tf_op jit(solution)/shard_map/combine/pallas_call | solution.py:615
  104.1 1.1 %copy.8 = f32[1,256,1280]{2,1,0:T(8,128)} copy(f32[1,256,1280]{2,1,0:T(8,128)S(1)} %bitcast.3) | data formatting | bytes 2621440
Async XLA Ops:
  0.6 63.4 %copy-start = (s32[1,256]{1,0:T(1,128)S(1)}, s32[1,256]{1,0:T(1,128)}, u32[]{:S(2)}) copy-start(s32[1,256]{1,0:T(1,128)} %lens_ref.1) | copy-start | bytes 3076

commit v7 on v6

--- a/solution.py
+++ b/solution.py
@@ -244,6 +244,19 @@
             value = acch[rows, pl.ds(part * D, D)] + jnp.dot(
                 nrmh[rows, others], wall[:, pl.ds((part + 1) * D, D)], preferred_element_type=F32
             )
+            for j in range(2):
+                start = pl.multiple_of(base + 128 * first + 256 * j, 128)
+                ref[pl.ds(start, 128), :] = value[128 * j : 128 * j + 128].astype(BF16)
+
+    def halo_whole(src, first, base):
+        for j in range(4):
+            at = 128 * first + 64 * (j % 2) + 256 * (j // 2)
+            nrmh[pl.ds(64 * j, 64), :] = normalize(src[pl.ds(at, 64), :], gain)
+        rows = pl.ds(0, 256)
+        for part, ref in ((1, ks), (2, vs)):
+            cols = pl.ds(part * D, D)
+            value = jnp.dot(nrmh[rows, mine], wown[:, cols], preferred_element_type=F32)
+            value = value + jnp.dot(nrmh[rows, others], wall[:, cols], preferred_element_type=F32)
             for j in range(2):
                 start = pl.multiple_of(base + 128 * first + 256 * j, 128)
                 ref[pl.ds(start, 128), :] = value[128 * j : 128 * j + 128].astype(BF16)
@@ -302,8 +315,7 @@
         halo.arrived(2)
         halo.arrived(3)
     with jax.named_scope("g13"):
-        halo_first(far, 1, 0)
-        halo_second(1, far_at, 0)
+        halo_whole(far, 1, far_at)
         weights.sent()
         halo.sent()
 
@@ -407,7 +419,7 @@
                 keys = pl.ds(start, n)
                 bias[:, pl.ds(0, n)] = jnp.where(ids == kid[:, keys], 0.0, -1e30)
 
-                several = 8 if size < 6 else 4
+                several = 8
 
                 def pairs(group, _):
                     work, soft = {}, {}

time: 105 us -> 104 us (level)
    pallas_call x1, Pallas kernels: 26.8 us -> 28.3 us  [combine(): pl.pallas_call(combine_kernel, name='combine', out_shape=pltpu.VMEM((IMAG...]
    pallas_call x1, Pallas kernels: 13.2 us -> 12.1 us  [attend(): pl.pallas_call(attend_kernel, name='attend', out_shape=(jax.ShapeDtypeStr...]
where the time goes in v7:
time: 104 us; the launch traced here: 105 us
  Pallas kernels  103 us (99%)
  local copies, waits for them, and re-layouts  1.06 us (1%)
    pallas_call x1, Pallas kernels, gather(): pl.pallas_call(gather_kernel, name='gather', out_shape=(pltpu.VMEM((N, D)...  62.6 us
    pallas_call x1, Pallas kernels, combine(): pl.pallas_call(combine_kernel, name='combine', out_shape=pltpu.VMEM((IMAG...  28.3 us
    pallas_call x1, Pallas kernels, attend(): pl.pallas_call(attend_kernel, name='attend', out_shape=(jax.ShapeDtypeStr...  12.1 us

profile of v7, /device:TPU:1, one launch (start us, length us, event | category | flops | bytes accessed | tf_op | source)
XLA Modules:
  0.0 104.8 jit_solution(5166524237452873171)
XLA Ops:
  0.6 0.0 copy-start
  0.6 62.6 %gather.1 = (bf16[512,1280]{1,0:T(8,128)(2,1)S(1)}, bf16[1536,1280]{1,0:T(8,128)(2,1)S(1)}, bf16[1536,1280]{1,0:T(8,128)(2,1)S(1)}, bf16[640,5120]{1,0:T(8,128)(2,1)S(1)}) custom-call(bf16[512,1280]{1,0:T(8,128)(2,1)} %bitcast.4, f32[1280]{0:T(1024)} %gain_ref.1, bf16[640,3840]{1,0:T(8,128)(2,1)} %wq_hbm.1, bf16[640,1280]{1,0:T(8,128)(2,1)} %wa_hbm.1), custom_call_target="tpu_custom_call" | custom-call | tf_op jit(solution)/shard_map/gather/pallas_call | solution.py:335
  63.3 0.0 copy-done
  63.3 12.1 %attend.1 = (bf16[512,1280]{1,0:T(8,128)(2,1)}, bf16[256,1280]{1,0:T(8,128)(2,1)S(1)}) custom-call(s32[1,256]{1,0:T(1,128)S(1)} %copy-done, bf16[512,1280]{1,0:T(8,128)(2,1)S(1)} %get-tuple-element.8.q, bf16[1536,1280]{1,0:T(8,128)(2,1)S(1)} %get-tuple-element.9.k, bf16[1536,1280]{1,0:T(8,128)(2,1)S(1)} %get-tuple-element.10.v, ...), custom_call_target="tpu_custom_call" | custom-call | tf_op jit(solution)/shard_map/attend/pallas_call | solution.py:503
  75.4 28.3 %combine.1 = f32[256,1280]{1,0:T(8,128)S(1)} custom-call(bf16[256,1280]{1,0:T(8,128)(2,1)S(1)} %get-tuple-element.13.part), custom_call_target="tpu_custom_call" | custom-call | tf_op jit(solution)/shard_map/combine/pallas_call | solution.py:627
  103.7 1.1 %copy.8 = f32[1,256,1280]{2,1,0:T(8,128)} copy(f32[1,256,1280]{2,1,0:T(8,128)S(1)} %bitcast.3) | data formatting | bytes 2621440
Async XLA Ops:
  0.6 62.6 %copy-start = (s32[1,256]{1,0:T(1,128)S(1)}, s32[1,256]{1,0:T(1,128)}, u32[]{:S(2)}) copy-start(s32[1,256]{1,0:T(1,128)} %lens_ref.1) | copy-start | bytes 3076
